TPU v7x, 256 devices: a whole 4x4x8 slice. The times are simulated.
256 devices in a mesh: row: 8 (over y, core), col: 32 (over x, z).
Axes of the slice: x: 4, y: 4, z: 8, core: 2. Of those that a mesh axis runs over, the one named last changes fastest.
Arguments:
- weights: float32 [40, 2048, 4096], P(None, 'row', 'col'), may hold values from -0.006214806 to 0.006214806
- pool: float32 [12, 2048, 4096], P(None, 'row', 'col'), may hold values from -6 to 6
- desired: float32 [12, 8], replicated, may hold values from -6 to 6
- plan: int32 [2, 16], replicated, may hold values from 0 to 11
- beam_ref: int32 [40], replicated, may hold values from 0 to 7
- step_size: float32 [40], replicated, may hold values from 0.2 to 0.8
- smoothing: float32 [40], replicated, may hold values from 0.05 to 0.2
- active: int32 [40], replicated, may hold values from 1 to 2
Outputs:
- final_weights: float32 [40, 2048, 4096], P(None, 'row', 'col')
- errors: float32 [2, 40, 16], replicated
Inputs may be any that keep to these rules, and one draw needn't show every extreme that they name: `plan`: indices of recorded snapshots. `beam_ref`: indices of reference signals.
All inputs are finite; a program needn't handle non-finite values.
Results may differ from a plain program's by a relative error of at most 0.00017.
Values sent between devices are 32-bit elements; how exact they have to be, the bound alone decides.
No kernel may reach another device: no remote copies, remote signals or barrier semaphores. Data moves between devices by JAX's collectives and lax.ppermute only.
A program may use at most 128 MiB of HBM per device.

v0:
```python
import functools
import math

import jax
import jax.numpy as jnp
from jax import lax
from jax.sharding import Mesh
from jax.sharding import PartitionSpec as P

NR = 2048
NC = 4096
ITERS = 2
ROW_COL = ("row_0", "row_1", "col_0", "col_1")
ROW = ("row_0", "row_1")
COL = ("col_0", "col_1")


def by_axis(value, axes):
    return functools.reduce(lax.psum, axes, value)


def extended(value, sides, width):
    edges = {}
    for axis, dim in sides:
        count, length = (lax.axis_size(axis), value.shape[dim])
        up = [(i, (i + 1) % count) for i in range(count - 1)]
        last = lax.slice_in_dim(value, length - width, length, axis=dim)
        leading = lax.slice_in_dim(value, 0, width, axis=dim)
        edges[dim] = (
            lax.ppermute(last, axis, up),
            lax.ppermute(leading, axis, [(b, a) for a, b in up]),
        )
    done = []
    for _, dim in sides:
        low, high = edges[dim]
        around = [(width, width) if d in done else (0, 0) for d in range(value.ndim)]
        value = jnp.concatenate([jnp.pad(low, around), value, jnp.pad(high, around)], axis=dim)
        done.append(dim)
    return value


def stencil(padded):
    center = padded[:, 1:-1, 1:-1]
    return (
        padded[:, 2:, 1:-1]
        + padded[:, :-2, 1:-1]
        + padded[:, 1:-1, 2:]
        + padded[:, 1:-1, :-2]
        - 4.0 * center
    )


def beam_sum(inner, snaps, scale):
    local = jnp.dot(
        inner.reshape(inner.shape[0], -1),
        snaps.reshape(snaps.shape[0], -1).T,
        precision=lax.Precision.HIGHEST,
    )
    return by_axis(local, ROW_COL) * scale


def body(weights, pool, desired, plan, beam_ref, step_size, smoothing, active):
    count = pool.shape[0]
    scale = 1.0 / math.sqrt(NR * NC)
    refs = desired.shape[1]
    pick = (beam_ref[:, None] == jnp.arange(refs, dtype=jnp.int32)[None, :]).astype(jnp.float32)
    targets = jnp.dot(pick, desired.T, precision=lax.Precision.HIGHEST)
    rate = (step_size * scale)[:, None, None]
    smooth = smoothing[:, None, None]
    history = []
    current = weights
    for step in range(ITERS):
        snaps = jnp.take(pool, plan[step], axis=0)
        beam_out = beam_sum(current, snaps, scale)
        padded = extended(current, ((ROW, 1), (COL, 2)), 1)
        lap = stencil(padded)
        select = (plan[step][None, :] == jnp.arange(count, dtype=jnp.int32)[:, None]).astype(
            jnp.float32
        )
        error = jnp.dot(targets, select, precision=lax.Precision.HIGHEST) - beam_out
        history.append(error)
        grad = jnp.dot(
            error, snaps.reshape(snaps.shape[0], -1), precision=lax.Precision.HIGHEST
        ).reshape(current.shape)
        live = (active > step).astype(jnp.float32)[:, None, None]
        current = current + live * (rate * grad + smooth * lap)
    return (current, jnp.stack(history))


def solution(mesh):
    split = Mesh(mesh.devices.reshape(4, 2, 4, 8), ("row_0", "row_1", "col_0", "col_1"))
    in_specs = (P(None, ROW, COL), P(None, ROW, COL), P(), P(), P(), P(), P(), P())
    out_specs = (P(None, ROW, COL), P())
    return jax.shard_map(body, mesh=split, in_specs=in_specs, out_specs=out_specs, check_vma=False)
```

profile of v0, /device:TPU:32, one launch (start us, length us, event | category | flops | bytes accessed | tf_op | source)
XLA Modules:
  0.0 224.7 jit_solution(8768315274296020385)
XLA Ops:
  0.6 0.0 copy-start
  0.6 0.0 copy-start.2
  0.7 5.7 %copy.51 = f32[40,256,128]{2,0,1:T(8,128)S(1)} copy(f32[40,256,128]{2,1,0:T(8,128)} %param.10) | data formatting | bytes 10485760 | tf_op args[0]
  6.3 2.3 %copy-done.6 = f32[40,256,128]{2,0,1:T(8,128)} copy-done((f32[40,256,128]{2,0,1:T(8,128)}, f32[40,256,128]{2,0,1:T(8,128)S(1)}, u32[]{:S(2)}) %copy-start.6) | copy-done | bytes 5242904
  8.7 1.7 collective-permute-start.1
  10.4 1.3 collective-permute-start
  11.7 5.8 %fusion.41 = (f32[40,256,1]{2,1,0:T(8,128)}, f32[40,256,1]{2,1,0:T(8,128)}) fusion(f32[40,256,128]{2,1,0:T(8,128)S(1)} %copy-done.2), kind=kLoop, calls=%fused_computation.79 | loop fusion | bytes 163840 | tf_op jit(solution)/shard_map/slice | solution.py:28
  17.5 3.3 %copy.59 = f32[40,256,1]{1,0,2:T(8,128)S(1)} copy(f32[40,256,1]{2,1,0:T(8,128)} %get-tuple-element.17) | data formatting | bytes 81920
  20.9 3.3 %collective-permute-start.2 = (f32[40,256,1]{1,0,2:T(8,128)S(1)}, f32[40,256,1]{1,0,2:T(8,128)S(1)}, u32[]{:S(2)}, u32[]{:S(2)}) collective-permute-start(f32[40,256,1]{1,0,2:T(8,128)S(1)} %copy.59), channel_id=1, source_target_pairs={{1,0},{2,1},{3,2},{4,3},{5,4},{6,5},{7,6},{8,7},{9,8},{10,9},{11,1... | collective-permute-start | bytes 122888 | tf_op jit(solution)/shard_map/ppermute | solution.py:31
  24.1 3.3 %copy.60 = f32[40,256,1]{1,0,2:T(8,128)S(1)} copy(f32[40,256,1]{2,1,0:T(8,128)} %get-tuple-element.18) | data formatting | bytes 81920
  27.5 2.6 %collective-permute-start.3 = (f32[40,256,1]{1,0,2:T(8,128)S(1)}, f32[40,256,1]{1,0,2:T(8,128)S(1)}, u32[]{:S(2)}, u32[]{:S(2)}) collective-permute-start(f32[40,256,1]{1,0,2:T(8,128)S(1)} %copy.60), channel_id=1, source_target_pairs={{0,1},{1,2},{2,3},{3,4},{4,5},{5,6},{6,7},{7,8},{8,9},{9,10},{10,1... | collective-permute-start | bytes 122888 | tf_op jit(solution)/shard_map/ppermute | solution.py:30
  30.1 2.0 gather_fusion
  32.1 1.9 broadcast_select_fusion.1
  34.0 1.3 copy-done.5
  35.3 10.3 %fusion.26 = f32[40,16]{0,1:T(8,128)S(1)} fusion(f32[16,256,128]{2,1,0:T(8,128)S(1)} %broadcast_select_fusion.1, f32[40,256,128]{2,1,0:T(8,128)} %param.10), kind=kOutput, calls=%fused_computation.46 | convolution fusion | flops 251658240 | bytes 7342592 | tf_op jit(solution)/shard_map/dot_general | solution.py:54
  45.7 13.4 %psum.56 = f32[40,16]{0,1:T(8,128)S(1)} all-reduce(f32[40,16]{0,1:T(8,128)S(1)} %fusion.26), channel_id=1, replica_groups=mesh['row_0'=4,'row_1'=2,'col_0'=4,'col_1'=8] {'row_0'}, use_global_device_ids=true, to_apply=%region_0.0 | all-reduce | flops 640 | bytes 5120 | tf_op jit(solution)/shard_map/psum | solution.py:19
  59.1 2.5 %psum.57 = f32[40,16]{0,1:T(8,128)S(1)} all-reduce(f32[40,16]{0,1:T(8,128)S(1)} %psum.56), channel_id=1, replica_groups=mesh['row_0'=4,'row_1'=2,'col_0'=4,'col_1'=8] {'row_1'}, use_global_device_ids=true, to_apply=%region_1.3 | all-reduce | flops 640 | bytes 5120 | tf_op jit(solution)/shard_map/psum | solution.py:19
  61.6 10.6 %psum.58 = f32[40,16]{0,1:T(8,128)S(1)} all-reduce(f32[40,16]{0,1:T(8,128)S(1)} %psum.57), channel_id=1, replica_groups=mesh['row_0'=4,'row_1'=2,'col_0'=4,'col_1'=8] {'col_0'}, use_global_device_ids=true, to_apply=%region_2.4 | all-reduce | flops 640 | bytes 5120 | tf_op jit(solution)/shard_map/psum | solution.py:19
  72.2 18.8 %psum.59 = f32[40,16]{0,1:T(8,128)S(1)} all-reduce(f32[40,16]{0,1:T(8,128)S(1)} %psum.58), channel_id=1, replica_groups=mesh['row_0'=4,'row_1'=2,'col_0'=4,'col_1'=8] {'col_1'}, use_global_device_ids=true, to_apply=%region_3.5 | all-reduce | flops 640 | bytes 5120 | tf_op jit(solution)/shard_map/psum | solution.py:19
  91.0 2.0 gather_fusion.1
  93.0 0.2 fusion.32
  93.2 3.2 %broadcast_select_fusion = f32[16,256,128]{2,1,0:T(8,128)} fusion(f32[16,256,128]{2,1,0:T(8,128)} %gather_fusion.1, pred[16]{0:T(512)(128)(4,1)S(1)} %get-tuple-element.9), kind=kLoop, calls=%fused_computation.50 | loop fusion | flops 524288 | bytes 4194320 | tf_op jit(solution)/shard_map/jit(_take)/select_n | solution.py:73
  96.4 0.2 convolution_subtract_fusion.1
  96.6 0.6 constant_dynamic-update-slice_fusion.2
  97.2 7.8 %constant_dynamic-update-slice_fusion.1 = f32[40,258,128]{2,0,1:T(8,128)} fusion(f32[40,258,128]{2,0,1:T(8,128)} %constant_dynamic-update-slice_fusion.2, f32[40,256,128]{2,1,0:T(8,128)} %param.10), kind=kLoop, calls=%fused_computation.61 | loop fusion | bytes 10485760
  105.1 0.6 constant_dynamic-update-slice_fusion
  105.7 3.2 %copy.47 = f32[40,256,1]{2,0,1:T(8,128)} copy(f32[40,256,1]{1,0,2:T(8,128)S(1)} %collective-permute-done.2) | data formatting | bytes 81920 | tf_op jit(solution)/shard_map/ppermute | solution.py:31
  108.8 3.1 %copy.49 = f32[40,256,1]{2,0,1:T(8,128)} copy(f32[40,256,1]{1,0,2:T(8,128)S(1)} %collective-permute-done.3) | data formatting | bytes 81920 | tf_op jit(solution)/shard_map/ppermute | solution.py:30
  112.0 18.1 %fusion.15 = f32[40,256,128]{2,0,1:T(8,128)S(1)} fusion(f32[40,256,128]{2,0,1:T(8,128)} %copy-done.6, f32[40,258,128]{2,0,1:T(8,128)} %constant_dynamic-update-slice_fusion, f32[40,256,1]{2,0,1:T(8,128)} %copy.49, f32[40,256,1]{2,0,1:T(8,128)} %copy.47, f32[40,1,128]{2,0,1:T(8,128)S(1)} %collective-permute-done.1, ...), kind=kOutput, calls=%fused_computation.26 | convolution fusion | flops 277872640 | bytes 17992672 | tf_op jit(solution)/shard_map/dot_general | solution.py:82
  130.1 5.5 %fusion.39 = (f32[40,256,1]{2,0,1:T(8,128)}, f32[40,256,1]{2,0,1:T(8,128)}) fusion(f32[40,256,128]{2,0,1:T(8,128)S(1)} %fusion.15), kind=kLoop, calls=%fused_computation.77 | loop fusion | bytes 163840 | tf_op jit(solution)/shard_map/slice | solution.py:28
  135.6 0.1 copy-done.3
  135.7 5.0 %fusion.29 = f32[40,16]{0,1:T(8,128)S(1)} fusion(f32[40,256,128]{2,0,1:T(8,128)S(1)} %fusion.15, f32[16,256,128]{2,1,0:T(8,128)S(1)} %copy-done.4), kind=kOutput, calls=%fused_computation.47 | convolution fusion | flops 251658240 | bytes 7342592 | tf_op jit(solution)/shard_map/dot_general | solution.py:54
  140.7 7.8 %psum.60 = f32[40,16]{0,1:T(8,128)S(1)} all-reduce(f32[40,16]{0,1:T(8,128)S(1)} %fusion.29), channel_id=1, replica_groups=mesh['row_0'=4,'row_1'=2,'col_0'=4,'col_1'=8] {'row_0'}, use_global_device_ids=true, to_apply=%region_4.6 | all-reduce | flops 640 | bytes 5120 | tf_op jit(solution)/shard_map/psum | solution.py:19
  148.5 2.5 %psum.61 = f32[40,16]{0,1:T(8,128)S(1)} all-reduce(f32[40,16]{0,1:T(8,128)S(1)} %psum.60), channel_id=1, replica_groups=mesh['row_0'=4,'row_1'=2,'col_0'=4,'col_1'=8] {'row_1'}, use_global_device_ids=true, to_apply=%region_5.7 | all-reduce | flops 640 | bytes 5120 | tf_op jit(solution)/shard_map/psum | solution.py:19
  151.0 8.1 %psum.62 = f32[40,16]{0,1:T(8,128)S(1)} all-reduce(f32[40,16]{0,1:T(8,128)S(1)} %psum.61), channel_id=1, replica_groups=mesh['row_0'=4,'row_1'=2,'col_0'=4,'col_1'=8] {'col_0'}, use_global_device_ids=true, to_apply=%region_6.8 | all-reduce | flops 640 | bytes 5120 | tf_op jit(solution)/shard_map/psum | solution.py:19
  159.1 17.6 %psum.63 = f32[40,16]{0,1:T(8,128)S(1)} all-reduce(f32[40,16]{0,1:T(8,128)S(1)} %psum.62), channel_id=1, replica_groups=mesh['row_0'=4,'row_1'=2,'col_0'=4,'col_1'=8] {'col_1'}, use_global_device_ids=true, to_apply=%region_7.9 | all-reduce | flops 640 | bytes 5120 | tf_op jit(solution)/shard_map/psum | solution.py:19
  176.8 3.5 %copy.54 = f32[40,256,1]{1,0,2:T(8,128)S(1)} copy(f32[40,256,1]{2,0,1:T(8,128)} %get-tuple-element.13) | data formatting | bytes 81920 | tf_op jit(solution)/shard_map/slice | solution.py:28
  180.3 1.9 collective-permute-start.6
  182.2 3.3 %copy.56 = f32[40,256,1]{1,0,2:T(8,128)S(1)} copy(f32[40,256,1]{2,0,1:T(8,128)} %get-tuple-element.14) | data formatting | bytes 81920 | tf_op jit(solution)/shard_map/slice | solution.py:27
  185.5 3.9 %collective-permute-start.7 = (f32[40,256,1]{1,0,2:T(8,128)S(1)}, f32[40,256,1]{1,0,2:T(8,128)S(1)}, u32[]{:S(2)}, u32[]{:S(2)}) collective-permute-start(f32[40,256,1]{1,0,2:T(8,128)S(1)} %copy.56), channel_id=1, source_target_pairs={{0,1},{1,2},{2,3},{3,4},{4,5},{5,6},{6,7},{7,8},{8,9},{9,10},{10,1... | collective-permute-start | bytes 122888 | tf_op jit(solution)/shard_map/ppermute | solution.py:30
  189.5 1.3 collective-permute-start.4
  190.8 3.0 %collective-permute-start.5 = (f32[40,1,128]{2,0,1:T(8,128)S(1)}, f32[40,1,128]{2,0,1:T(8,128)S(1)}, u32[]{:S(2)}, u32[]{:S(2)}) collective-permute-start(f32[40,1,128]{2,0,1:T(8,128)S(1)} %get-tuple-element.15), channel_id=1, source_target_pairs={{0,32},{32,64},{64,96},{96,128},{128,160},{160,192},{192,224},{1,3... | collective-permute-start | bytes 61448 | tf_op jit(solution)/shard_map/ppermute | solution.py:30
  193.8 0.2 convolution_subtract_fusion
  194.0 0.6 pad_maximum_fusion.10
  194.6 3.1 %copy.55 = f32[40,256,1]{2,0,1:T(8,128)} copy(f32[40,256,1]{1,0,2:T(8,128)S(1)} %collective-permute-done.6) | data formatting | bytes 81920 | tf_op jit(solution)/shard_map/ppermute | solution.py:31
  197.7 3.1 %copy.57 = f32[40,256,1]{2,0,1:T(8,128)} copy(f32[40,256,1]{1,0,2:T(8,128)S(1)} %collective-permute-done.7) | data formatting | bytes 81920 | tf_op jit(solution)/shard_map/ppermute | solution.py:30
  200.8 20.5 %fusion.6 = f32[40,256,128]{2,0,1:T(8,128)S(1)} fusion(f32[40,256,128]{2,0,1:T(8,128)} %copy-done.3, f32[40,256,1]{2,0,1:T(8,128)} %copy.57, f32[40,1,128]{2,0,1:T(8,128)S(1)} %collective-permute-done.4, f32[40,1,128]{2,0,1:T(8,128)S(1)} %collective-permute-done.5, f32[40,256,1]{2,0,1:T(8,128)} %copy.55, f32[40]{0:T(128)S(1)} %get-tuple-element.25, ...), kind=kOutput, calls=%fused_computation.9 | convolution fusion | flops 283115520 | bytes 12708832 | tf_op jit(solution)/shard_map/dot_general | solution.py:82
  221.4 3.3 %copy.58 = f32[40,256,128]{2,1,0:T(8,128)} copy(f32[40,256,128]{2,0,1:T(8,128)S(1)} %fusion.6) | data formatting | bytes 10485760
  (37 shorter events, 0.1 us)
Async XLA Ops:
  0.6 29.5 %copy-start = (f32[12,256,128]{2,1,0:T(8,128)S(1)}, f32[12,256,128]{2,1,0:T(8,128)}, u32[]{:S(2)}) copy-start(f32[12,256,128]{2,1,0:T(8,128)} %param.11) | copy-start | bytes 4718596
  0.6 11.1 %copy-start.2 = (f32[40,256,128]{2,1,0:T(8,128)S(1)}, f32[40,256,128]{2,1,0:T(8,128)}, u32[]{:S(2)}) copy-start(f32[40,256,128]{2,1,0:T(8,128)} %param.10) | copy-start | bytes 15728644
  6.3 2.4 %copy-start.6 = (f32[40,256,128]{2,0,1:T(8,128)}, f32[40,256,128]{2,0,1:T(8,128)S(1)}, u32[]{:S(2)}) copy-start(f32[40,256,128]{2,0,1:T(8,128)S(1)} %copy.51) | copy-start | bytes 15728644
  8.7 87.9 %collective-permute-start.1 = (f32[40,1,128]{2,0,1:T(8,128)S(1)}, f32[40,1,128]{2,0,1:T(8,128)S(1)}, u32[]{:S(2)}, u32[]{:S(2)}) collective-permute-start(f32[40,1,128]{2,0,1:T(8,128)S(1)} %get-tuple-element.20), channel_id=1, source_target_pairs={{0,32},{32,64},{64,96},{96,128},{128,160},{160,192},{192,224},{1,3... | collective-permute-start | bytes 61448 | tf_op jit(solution)/shard_map/ppermute | solution.py:30
  10.4 94.6 %collective-permute-start = (f32[40,1,128]{2,0,1:T(8,128)S(1)}, f32[40,1,128]{2,0,1:T(8,128)S(1)}, u32[]{:S(2)}, u32[]{:S(2)}) collective-permute-start(f32[40,1,128]{2,0,1:T(8,128)S(1)} %get-tuple-element.19), channel_id=1, source_target_pairs={{32,0},{64,32},{96,64},{128,96},{160,128},{192,160},{224,192},{33,... | collective-permute-start | bytes 61448 | tf_op jit(solution)/shard_map/ppermute | solution.py:31
  17.5 12.5 %copy-start.7 = (s32[2,16]{1,0:T(2,128)S(1)}, s32[2,16]{1,0:T(2,128)}, u32[]{:S(2)}) copy-start(s32[2,16]{1,0:T(2,128)} %param.13) | copy-start | bytes 388
  20.9 84.8 %collective-permute-start.2 = (f32[40,256,1]{1,0,2:T(8,128)S(1)}, f32[40,256,1]{1,0,2:T(8,128)S(1)}, u32[]{:S(2)}, u32[]{:S(2)}) collective-permute-start(f32[40,256,1]{1,0,2:T(8,128)S(1)} %copy.59), channel_id=1, source_target_pairs={{1,0},{2,1},{3,2},{4,3},{5,4},{6,5},{7,6},{8,7},{9,8},{10,9},{11,1... | collective-permute-start | bytes 122888 | tf_op jit(solution)/shard_map/ppermute | solution.py:31
  27.5 81.4 %collective-permute-start.3 = (f32[40,256,1]{1,0,2:T(8,128)S(1)}, f32[40,256,1]{1,0,2:T(8,128)S(1)}, u32[]{:S(2)}, u32[]{:S(2)}) collective-permute-start(f32[40,256,1]{1,0,2:T(8,128)S(1)} %copy.60), channel_id=1, source_target_pairs={{0,1},{1,2},{2,3},{3,4},{4,5},{5,6},{6,7},{7,8},{8,9},{9,10},{10,1... | collective-permute-start | bytes 122888 | tf_op jit(solution)/shard_map/ppermute | solution.py:30
  32.1 58.8 %copy-start.9 = (s32[40]{0:T(128)S(1)}, s32[40]{0:T(128)}, u32[]{:S(2)}) copy-start(s32[40]{0:T(128)} %param.17) | copy-start | bytes 484
  34.0 1.3 copy-start.5
  35.3 57.7 %copy-start.8 = (f32[12,8]{0,1:T(8,128)S(1)}, f32[12,8]{0,1:T(8,128)}, u32[]{:S(2)}) copy-start(f32[12,8]{0,1:T(8,128)} %param.12) | copy-start | bytes 1156
  35.3 57.7 %copy-start.10 = (s32[40]{0:T(128)S(1)}, s32[40]{0:T(128)}, u32[]{:S(2)}) copy-start(s32[40]{0:T(128)} %param.14) | copy-start | bytes 484
  45.7 50.9 %copy-start.11 = (f32[40]{0:T(128)S(1)}, f32[40]{0:T(128)}, u32[]{:S(2)}) copy-start(f32[40]{0:T(128)} %param.15) | copy-start | bytes 484
  105.7 6.3 %copy-start.12 = (f32[40]{0:T(128)S(1)}, f32[40]{0:T(128)}, u32[]{:S(2)}) copy-start(f32[40]{0:T(128)} %param.16) | copy-start | bytes 484
  130.1 5.7 %copy-start.3 = (f32[40,256,128]{2,0,1:T(8,128)}, f32[40,256,128]{2,0,1:T(8,128)S(1)}, u32[]{:S(2)}) copy-start(f32[40,256,128]{2,0,1:T(8,128)S(1)} %fusion.15) | copy-start | bytes 15728644
  130.1 5.7 %copy-start.4 = (f32[16,256,128]{2,1,0:T(8,128)S(1)}, f32[16,256,128]{2,1,0:T(8,128)}, u32[]{:S(2)}) copy-start(f32[16,256,128]{2,1,0:T(8,128)} %broadcast_select_fusion) | copy-start | bytes 6291460
  180.3 14.3 %collective-permute-start.6 = (f32[40,256,1]{1,0,2:T(8,128)S(1)}, f32[40,256,1]{1,0,2:T(8,128)S(1)}, u32[]{:S(2)}, u32[]{:S(2)}) collective-permute-start(f32[40,256,1]{1,0,2:T(8,128)S(1)} %copy.54), channel_id=1, source_target_pairs={{1,0},{2,1},{3,2},{4,3},{5,4},{6,5},{7,6},{8,7},{9,8},{10,9},{11,1... | collective-permute-start | bytes 122888 | tf_op jit(solution)/shard_map/ppermute | solution.py:31
  185.5 12.2 %collective-permute-start.7 = (f32[40,256,1]{1,0,2:T(8,128)S(1)}, f32[40,256,1]{1,0,2:T(8,128)S(1)}, u32[]{:S(2)}, u32[]{:S(2)}) collective-permute-start(f32[40,256,1]{1,0,2:T(8,128)S(1)} %copy.56), channel_id=1, source_target_pairs={{0,1},{1,2},{2,3},{3,4},{4,5},{5,6},{6,7},{7,8},{8,9},{9,10},{10,1... | collective-permute-start | bytes 122888 | tf_op jit(solution)/shard_map/ppermute | solution.py:30
  189.5 11.4 %collective-permute-start.4 = (f32[40,1,128]{2,0,1:T(8,128)S(1)}, f32[40,1,128]{2,0,1:T(8,128)S(1)}, u32[]{:S(2)}, u32[]{:S(2)}) collective-permute-start(f32[40,1,128]{2,0,1:T(8,128)S(1)} %get-tuple-element.16), channel_id=1, source_target_pairs={{32,0},{64,32},{96,64},{128,96},{160,128},{192,160},{224,192},{33,... | collective-permute-start | bytes 61448 | tf_op jit(solution)/shard_map/ppermute | solution.py:31
  190.8 10.1 %collective-permute-start.5 = (f32[40,1,128]{2,0,1:T(8,128)S(1)}, f32[40,1,128]{2,0,1:T(8,128)S(1)}, u32[]{:S(2)}, u32[]{:S(2)}) collective-permute-start(f32[40,1,128]{2,0,1:T(8,128)S(1)} %get-tuple-element.15), channel_id=1, source_target_pairs={{0,32},{32,64},{64,96},{96,128},{128,160},{160,192},{192,224},{1,3... | collective-permute-start | bytes 61448 | tf_op jit(solution)/shard_map/ppermute | solution.py:30
  200.8 23.8 %copy-start.1 = (f32[12,256,128]{2,1,0:T(8,128)S(1)}, f32[12,256,128]{2,1,0:T(8,128)}, u32[]{:S(2)}) copy-start(f32[12,256,128]{2,1,0:T(8,128)} %param.11) | copy-start | bytes 4718596
where the time goes:
time: 228 us; the launch traced here: 225 us
  blocking collectives  81.3 us (36%)
  local copies, waits for them, and re-layouts  63.1 us (28%)
  matrix products  54.5 us (24%)
  starting transfers between devices  19 us (8%)
  other arithmetic  5.76 us (3%)
    psum x8, blocking collectives, by_axis(): return functools.reduce(lax.psum, axes, value)  81.3 us
    dot_general x2, matrix products, body(): jnp.dot(error, snaps.reshape(snaps.shape[0], -1), precision=lax.Precision...  38.6 us
    unnamed x32, local copies, waits for them, and re-layouts  27.8 us
    dot_general x2, matrix products, beam_sum(): jnp.dot(inner.reshape(inner.shape[0], -1), snaps.reshape(snaps.shape[0],...  15.3 us
    slice x4, local copies, waits for them, and re-layouts, extended(): leading = lax.slice_in_dim(value, 0, width, axis=dim)  14.9 us
    ppermute x4, starting transfers between devices, extended(): lax.ppermute(last, axis, up)  11.2 us
    ppermute x4, starting transfers between devices, extended(): lax.ppermute(leading, axis, [(b, a) for a, b in up])  7.79 us
    ppermute x2, local copies, waits for them, and re-layouts, extended(): lax.ppermute(leading, axis, [(b, a) for a, b in up])  6.29 us
  transfers between devices with their start and end apart: 8, of which 0 were waited for; matrix products, arithmetic and copies ran while one was open for 24% of the time, Pallas kernels for 0%

commit v1 on v0

v1 whole, which is shorter than its diff:
```python
import math

import jax
import jax.numpy as jnp
from jax import lax
from jax.experimental import pallas as pl
from jax.experimental.pallas import tpu as pltpu
from jax.sharding import Mesh
from jax.sharding import PartitionSpec as P

NR = 2048
NC = 4096
ROW = ("row_0", "row_1")
COL = ("col_0", "col_1")
NEAR = ("row_1", "col_1")
FAR = ("row_0", "col_0")
SCALE = 1.0 / math.sqrt(NR * NC)
BEAMS, POOL, ROWS, LANES = 40, 12, 256, 128
GROUP = 4
LIMIT = 30 << 20
EXACT = lax.Precision.HIGHEST
NN = (((1,), (0,)), ((), ()))
NT = (((1,), (1,)), ((), ()))
TN = (((0,), (0,)), ((), ()))
F32, BF16 = jnp.float32, jnp.bfloat16
VMEM = pl.BlockSpec(memory_space=pltpu.VMEM)
HBM = pl.BlockSpec(memory_space=pltpu.HBM)
SMEM = pl.BlockSpec(memory_space=pltpu.SMEM)


def iota(shape, dim):
    return lax.broadcasted_iota(jnp.int32, shape, dim)


def dot(a, b, dims, precision=None):
    return lax.dot_general(a, b, dims, precision=precision, preferred_element_type=F32)


def halves(x):
    high = x.astype(BF16)
    return high, (x - high.astype(F32)).astype(BF16)


def thirds(x):
    high = x.astype(BF16)
    rest = x - high.astype(F32)
    mid = rest.astype(BF16)
    return high, mid, (rest - mid.astype(F32)).astype(BF16)


def dot_exact(ones, x, dims):
    return sum(dot(ones.astype(BF16), part, dims) for part in thirds(x))


def exact_dot(x, ones, dims):
    return sum(dot(part, ones.astype(BF16), dims) for part in thirds(x))


def rows_around(x):
    zero = jnp.zeros((1, LANES), F32)
    return jnp.concatenate([x[1:], zero], axis=0) + jnp.concatenate([zero, x[:-1]], axis=0)


def band_matrix(center):
    away = jnp.abs(iota((LANES, LANES), 0) - iota((LANES, LANES), 1))
    return jnp.where(away == 0, center, jnp.where(away == 1, 1.0, 0.0))


def lap_inside(x, along):
    return rows_around(x) + dot(jnp.concatenate(halves(x), axis=1), along, NN)


def line_ends(w_hbm, pool_hbm, top_ref, bottom_ref, w_buf, pool_buf, sems):
    copies = []
    for k, at in enumerate((0, ROWS - 8)):
        for j, (src, dst) in enumerate(((w_hbm, w_buf), (pool_hbm, pool_buf))):
            copies.append(pltpu.make_async_copy(src.at[:, at : at + 8, :], dst.at[k], sems.at[2 * k + j]))
    for copy in copies:
        copy.start()
    for copy in copies:
        copy.wait()
    for k, (ref, near, far) in enumerate(((top_ref, 0, 1), (bottom_ref, 7, 6))):
        ref[0:40, :] = w_buf[k, :, near, :]
        ref[40:80, :] = w_buf[k, :, far, :]
        ref[80:96, :] = jnp.zeros((16, LANES), F32)
        ref[80:92, :] = pool_buf[k, :, near, :]


def column_ends(w_hbm, pool_hbm, left_ref, right_ref, w_buf, pool_buf, ends_ref, sems):
    copies = [pltpu.make_async_copy(pool_hbm, pool_buf, sems.at[5])]
    for k in range(5):
        copies.append(pltpu.make_async_copy(w_hbm.at[8 * k : 8 * k + 8], w_buf.at[8 * k : 8 * k + 8], sems.at[k]))
    for copy in copies:
        copy.start()
    row, lane = iota((8, LANES), 0), iota((8, LANES), 1)
    pick = jnp.zeros((8, LANES), F32)
    for k, spot in enumerate((0, LANES - 1, 1, LANES - 2)):
        pick = jnp.where((row == k) & (lane == spot), 1.0, pick)
    pick = pick.astype(BF16)
    pick = jnp.concatenate([pick, pick], axis=1)

    def taken(ref, first):
        def image(p, carry):
            ends_ref[first + p] = dot(pick, jnp.concatenate(halves(ref[p]), axis=1), NT)
            return carry

        return image

    copies[0].wait()
    lax.fori_loop(0, POOL, taken(pool_buf, BEAMS), 0, unroll=4)
    for k in range(5):
        copies[1 + k].wait()
        lax.fori_loop(8 * k, 8 * k + 8, taken(w_buf, 0), 0, unroll=4)
    for ref, near, far in ((left_ref, 0, 2), (right_ref, 1, 3)):
        ref[0:40, :] = ends_ref[0:40, near, :]
        ref[40:80, :] = ends_ref[0:40, far, :]
        ref[80:96, :] = jnp.zeros((16, ROWS), F32)
        ref[80:92, :] = ends_ref[40:52, near, :]


def gram(w_ref, pool_ref, sums_ref, lap_ref, acc_ref):
    along = band_matrix(-4.0).astype(BF16)
    along = jnp.concatenate([along, along], axis=0)
    acc_ref[...] = jnp.zeros_like(acc_ref)

    def smooth(p, carry):
        lap_ref[p] = lap_inside(pool_ref[p], along)
        return carry

    lax.fori_loop(0, POOL, smooth, 0, unroll=4)

    def pair(ref, count, t):
        parts = []
        for k in range(GROUP):
            at = pl.multiple_of(t * GROUP * 8 + k * 8, 8)
            parts.append(ref[:, pl.ds(at, 8), :].reshape(count * 8, LANES))
        return jnp.concatenate(parts, axis=1)

    def step(t, carry):
        p_high, p_low = halves(pair(pool_ref, POOL, t))
        l_high, l_low = halves(pair(lap_ref, POOL, t))
        w_high, w_low = halves(pair(w_ref, BEAMS, t))
        a_high = jnp.concatenate([w_high, p_high], axis=0)
        a_low = jnp.concatenate([w_low, p_low], axis=0)
        b_high = jnp.concatenate([p_high, l_high], axis=0)
        b_low = jnp.concatenate([p_low, l_low], axis=0)
        left = jnp.concatenate([a_high, a_high, a_low], axis=1)
        right = jnp.concatenate([b_high, b_low, b_high], axis=1)
        acc_ref[...] += dot(left, right, NT)
        return carry

    lax.fori_loop(0, 32 // GROUP, step, 0)
    n, m = acc_ref.shape
    same = (iota((n, m), 0) & 7) == (iota((n, m), 1) & 7)
    kept = jnp.where(same, acc_ref[...], 0.0)
    q, j = iota((32, m), 0), iota((32, m), 1) >> 3
    fold = jnp.where(((j < POOL) & (q == j)) | ((j >= POOL) & (q == j + 16 - POOL)), 1.0, 0.0)
    folded = dot_exact(fold, kept, NT)
    i, lane = iota((n, LANES), 0) >> 3, iota((n, LANES), 1)
    to_p = jnp.where(((i < BEAMS) & (lane == i)) | ((i >= BEAMS) & (lane == i + 80 - BEAMS)), 1.0, 0.0)
    to_l = jnp.where((i < BEAMS) & (lane == i + 40), 1.0, 0.0)
    sums = exact_dot(folded[0:16], to_p, NN) + exact_dot(folded[16:32], to_l, NN)
    sums_ref[...] = sums[0:POOL]


def again(parts_ref, out_ref):
    sums = parts_ref[0]
    for k in range(1, 16):
        sums = sums + parts_ref[k]
    for k in range(16):
        out_ref[k] = sums


def base(
    smooth_ref, active_ref, w_ref, pool_lap_ref, sums_ref, smooth_row_ref, active_row_ref,
    top_ref, bottom_ref, left_ref, right_ref, up_ref, down_ref, west_ref, east_ref,
    sent_ref, out_ref, lap_ref, fix_ref, p_fix_ref,
):
    halo = jnp.concatenate([ref[80:96, :] for ref in (west_ref, east_ref, up_ref, down_ref)], axis=1)
    edge = jnp.concatenate([ref[0:40, :] for ref in (left_ref, right_ref, top_ref, bottom_ref)], axis=1)
    edge = jnp.concatenate([jnp.zeros((40, 768), F32), edge, jnp.zeros((48, 768), F32)], axis=0)
    sums = sums_ref[...] + dot(halo, edge, NT, EXACT)[0:POOL]
    for k in range(16):
        sent_ref[k] = sums

    def across(row):
        return jnp.broadcast_to(row, (8, BEAMS)).T[:, 0:1]

    smooth_row, active_row = smooth_row_ref[...], active_row_ref[...]
    live0 = jnp.where(active_row > 0, 1.0, 0.0)
    live1 = jnp.where(active_row > 1, 1.0, 0.0)
    a = across(smooth_row * (live0 + live1))
    c = across(smooth_row * smooth_row * live0 * live1)
    r = lax.axis_index(ROW[0]) * 2 + lax.axis_index(ROW[1])
    k = lax.axis_index(COL[0]) * 8 + lax.axis_index(COL[1])
    has_up, has_down = jnp.where(r > 0, 1.0, 0.0), jnp.where(r < 7, 1.0, 0.0)
    has_west, has_east = jnp.where(k > 0, 1.0, 0.0), jnp.where(k < 31, 1.0, 0.0)
    span, shifted, corner = slice(0, 40), slice(40, 80), slice(96, 136)
    wide, thin = iota((BEAMS, ROWS), 1), iota((BEAMS, LANES), 1)

    def mixed(near, far, own, prev, after):
        return a * near + c * (2.0 * (prev + after) - 8.0 * near + far + own), c * near

    def column(msg_ref, own_ref, has):
        near = msg_ref[span, :]
        prev = jnp.where(wide == 0, 0.0, pltpu.roll(near, 1, 1))
        after = jnp.where(wide == ROWS - 1, 0.0, pltpu.roll(near, ROWS - 1, 1))
        return mixed(near, msg_ref[shifted, :], has * own_ref[span, :], prev, after)

    def line(msg_ref, own_ref, has, at):
        near = msg_ref[span, :]
        west = pltpu.roll(west_ref[corner, at : at + LANES], 1, 1)
        east = pltpu.roll(east_ref[corner, at : at + LANES], LANES - 1, 1)
        prev = jnp.where(thin == 0, west, pltpu.roll(near, 1, 1))
        after = jnp.where(thin == LANES - 1, east, pltpu.roll(near, LANES - 1, 1))
        return mixed(near, msg_ref[shifted, :], has * own_ref[span, :], prev, after)

    fix_ref[...] = jnp.zeros_like(fix_ref)
    fix_ref[:, 0, 0:256], fix_ref[:, 1, 0:256] = column(west_ref, left_ref, has_west)
    fix_ref[:, 2, 0:256], fix_ref[:, 3, 0:256] = column(east_ref, right_ref, has_east)
    fix_ref[:, 0, 256:384], fix_ref[:, 1, 256:384] = line(up_ref, top_ref, has_up, 0)
    fix_ref[:, 7, 384:512], fix_ref[:, 6, 384:512] = line(down_ref, bottom_ref, has_down, LANES)

    row, lane = iota((16, LANES), 0) & 7, iota((16, LANES), 1)
    place = jnp.zeros((16, LANES), F32)
    for k, spot in enumerate((0, 1, LANES - 1, LANES - 2)):
        place = jnp.where((row == k) & (lane == spot), 1.0, place)
    place = place.astype(BF16)

    def placed(x):
        high, low = halves(x)
        both = jnp.concatenate([high.astype(F32), low.astype(F32)], axis=0)
        return dot(both.T.astype(BF16), place, NN)

    p_fix_ref[...] = jnp.zeros_like(p_fix_ref)
    p_fix_ref[:, 0, :] = west_ref[80:92, :]
    p_fix_ref[:, 2, :] = east_ref[80:92, :]

    def pool_step(p, carry):
        lap_ref[p] = pool_lap_ref[p] + placed(p_fix_ref[p])
        return carry

    lax.fori_loop(0, POOL, pool_step, 0, unroll=4)
    lap_ref[:, 0, :] += up_ref[80:92, :]
    lap_ref[:, ROWS - 1, :] += down_ref[80:92, :]

    once = band_matrix(-2.0)
    twice = dot(once, once, NN)
    along = jnp.concatenate([once, twice], axis=1).astype(BF16)
    along = jnp.concatenate([along, along], axis=0)

    def beam(b, carry):
        x = w_ref[b]
        s_b, n_b = smooth_ref[b], active_ref[b]
        live0, live1 = jnp.where(n_b > 0, 1.0, 0.0), jnp.where(n_b > 1, 1.0, 0.0)
        a_b, c_b = s_b * (live0 + live1), s_b * s_b * live0 * live1
        sides = dot(jnp.concatenate(halves(x), axis=1), along, NN)
        one, two = sides[:, :LANES], sides[:, LANES:]
        down = rows_around(x) - 2.0 * x
        inner = a_b * x + c_b * (down + 2.0 * one)
        out = (x + a_b * one + c_b * two) + (rows_around(inner) - 2.0 * inner) + placed(fix_ref[b, :, 0:256])
        out_ref[b, 8 : ROWS - 8, :] = out[8 : ROWS - 8]
        out_ref[b, 0:8, :] = out[0:8] + fix_ref[b, :, 256:384]
        out_ref[b, ROWS - 8 : ROWS, :] = out[ROWS - 8 :] + fix_ref[b, :, 384:512]
        return carry

    lax.fori_loop(0, BEAMS, beam, 0, unroll=2)


def finish(
    parts_ref, desired_ref, plan_ref, ref_ref, rate_ref, smooth_ref, active_ref, base_ref, pool_ref, lap_ref,
    out_hbm, err_ref, done_ref, high_ref, low_ref, sems,
):
    def store(t):
        at = pl.ds(pl.multiple_of(t * 32, 8), 32)
        return pltpu.make_async_copy(done_ref.at[:, at, :], out_hbm.at[:, at, :], sems.at[t])

    sums = parts_ref[0]
    for k in range(1, 16):
        sums = sums + parts_ref[k]
    one_hot = jnp.where(iota((8, BEAMS), 0) == ref_ref[...], 1.0, 0.0)
    target = dot(desired_ref[...], one_hot, TN, EXACT)
    rate, smooth = rate_ref[...] * SCALE, smooth_ref[...]
    live0 = jnp.where(active_ref[...] > 0, 1.0, 0.0)
    live1 = jnp.where(active_ref[...] > 1, 1.0, 0.0)
    hits = [jnp.where(iota((POOL, 16), 0) == plan_ref[t : t + 1, :], 1.0, 0.0) for t in range(2)]
    many = [jnp.sum(h, axis=1, keepdims=True) for h in hits]
    p0 = sums[:, 0:BEAMS]
    lap = pltpu.roll(sums, LANES - 40, 1)[:, 0:BEAMS]
    inner = pltpu.roll(sums, LANES - 80, 1)[:, 0:POOL]
    e0 = target - SCALE * p0
    c0 = many[0] * e0
    p1 = p0 + live0 * (rate * dot(inner, c0, NN, EXACT) + smooth * lap)
    e1 = target - SCALE * p1
    c1 = many[1] * e1
    for t, e in enumerate((e0, e1)):
        err_ref[t] = dot(hits[t], e, TN, EXACT)
    d0 = rate * (live0 * c0 + live1 * c1)
    d1 = live0 * live1 * rate * smooth * c0
    gap = jnp.zeros((4, BEAMS), F32)
    both = jnp.concatenate([d0, gap, d1, gap], axis=0)
    spread = jnp.where((iota((320, BEAMS), 0) >> 3) == iota((320, BEAMS), 1), 1.0, 0.0)
    by_q = dot(spread, both, NT, EXACT)
    q, j = iota((32, 192), 0), iota((32, 192), 1) >> 3
    fold = jnp.where(((j < POOL) & (q == j)) | ((j >= POOL) & (q == j + 16 - POOL)), 1.0, 0.0)
    wide = dot(by_q, fold, NN, EXACT)
    same = (iota(wide.shape, 0) & 7) == (iota(wide.shape, 1) & 7)
    high, low = halves(jnp.where(same, wide, 0.0))
    high_ref[...] = high
    low_ref[...] = low

    def step(t, carry):
        def tile(ref, at):
            return ref.at[:, pl.ds(pl.multiple_of(t * 32 + at, 8), 8), :]

        for k in range(2):
            halves_of = []
            for h in range(2):
                at = 16 * k + 8 * h
                halves_of.append(
                    jnp.concatenate([tile(ref, at)[...].reshape(96, LANES) for ref in (pool_ref, lap_ref)], axis=0)
                )
            high, low = halves(jnp.concatenate(halves_of, axis=1))
            got = dot(high_ref[...], high, NN) + dot(high_ref[...], low, NN) + dot(low_ref[...], high, NN)
            for h in range(2):
                part = got[:, h * LANES : (h + 1) * LANES].reshape(BEAMS, 8, LANES)
                at = 16 * k + 8 * h
                tile(done_ref, at)[...] = tile(base_ref, at)[...] + part
        store(t).start()
        return carry

    lax.fori_loop(0, 8, step, 0)
    for t in range(8):
        store(t).wait()


def call(kernel, outs, specs, scratch=(), out_specs=None):
    run = pl.pallas_call(
        kernel,
        name=kernel.__name__,
        out_shape=outs,
        in_specs=specs,
        out_specs=out_specs or [VMEM] * len(outs),
        scratch_shapes=scratch,
        compiler_params=pltpu.CompilerParams(vmem_limit_bytes=LIMIT),
    )
    homes = {id(VMEM): pltpu.VMEM, id(HBM): pltpu.HBM}

    def at_home(value, spec):
        return pltpu.with_memory_space_constraint(value, homes[id(spec)]) if id(spec) in homes else value

    return lambda *args: run(*[at_home(x, spec) for x, spec in zip(args, specs)])


def vmem(*dims):
    return pltpu.VMEM(dims, F32)


def far_out(*dims):
    return pltpu.HBM(dims, F32)


def moved(value, axes, ahead):
    count = lax.axis_size(axes)
    pairs = [(i, i + 1) for i in range(count - 1)]
    return lax.ppermute(value, axes, pairs if ahead else [(b, a) for a, b in pairs])


def exchange(value, axes):
    return lax.all_to_all(value, axes, split_axis=0, concat_axis=0, tiled=True)


def body(weights, pool, desired, plan, beam_ref, step_size, smoothing, active):
    DMA = pltpu.SemaphoreType.DMA
    top, bottom = call(
        line_ends,
        [vmem(96, LANES)] * 2,
        [HBM, HBM],
        [vmem(2, BEAMS, 8, LANES), vmem(2, POOL, 8, LANES), DMA((4,))],
    )(weights, pool)
    from_up = moved(bottom, ROW, True)
    from_down = moved(top, ROW, False)
    left, right, w_near, p_near = call(
        column_ends,
        [vmem(96, ROWS)] * 2 + [vmem(BEAMS, ROWS, LANES), vmem(POOL, ROWS, LANES)],
        [HBM, HBM],
        [vmem(BEAMS + POOL, 8, ROWS), DMA((6,))],
    )(weights, pool)
    corners = jnp.concatenate([from_up[0:40], from_down[0:40]], axis=1)
    from_west = moved(jnp.concatenate([right, corners], axis=0), COL, True)
    from_east = moved(jnp.concatenate([left, corners], axis=0), COL, False)
    sums, pool_lap = call(
        gram, [vmem(POOL, LANES), vmem(POOL, ROWS, LANES)], [VMEM, VMEM], [vmem(416, 192)]
    )(w_near, p_near)
    rows = (smoothing[None, :], active[None, :])
    sent, based, lap = call(
        base,
        [vmem(16, POOL, LANES), vmem(BEAMS, ROWS, LANES), vmem(POOL, ROWS, LANES)],
        [SMEM, SMEM] + [VMEM] * 13,
        [vmem(BEAMS, 8, 512), vmem(POOL, 8, ROWS)],
    )(
        smoothing, active, w_near, pool_lap, sums, *rows,
        top, bottom, left, right, from_up, from_down, from_west, from_east,
    )
    near = exchange(sent, NEAR)
    (sent,) = call(again, [vmem(16, POOL, LANES)], [VMEM])(near)
    far = exchange(sent, FAR)
    final, errors = call(
        finish,
        [far_out(BEAMS, ROWS, LANES), vmem(2, 16, BEAMS)],
        [VMEM] * 10,
        [
            vmem(BEAMS, ROWS, LANES),
            pltpu.VMEM((320, 192), BF16),
            pltpu.VMEM((320, 192), BF16),
            DMA((8,)),
        ],
        [HBM, VMEM],
    )(far, desired.T, plan, beam_ref[None, :], step_size[None, :], *rows, based, p_near, lap)
    return final, jnp.swapaxes(errors, 1, 2)


def solution(mesh):
    split = Mesh(mesh.devices.reshape(4, 2, 4, 8), ("row_0", "row_1", "col_0", "col_1"))
    in_specs = (P(None, ROW, COL), P(None, ROW, COL), P(), P(), P(), P(), P(), P())
    out_specs = (P(None, ROW, COL), P())
    return jax.shard_map(body, mesh=split, in_specs=in_specs, out_specs=out_specs, check_vma=False)
```

time: 228 us -> 70.6 us (0.31); the launches traced: 225 us -> 70.3 us
  local copies, waits for them, and re-layouts: 63.1 us -> 0.65 us
  matrix products: 54.5 us -> 0 us
  blocking collectives: 81.3 us -> 32.3 us
  Pallas kernels: 0 us -> 26.3 us
  starting transfers between devices: 19 us -> 10.2 us
  other arithmetic: 5.76 us -> 0.02 us
    psum x8 -> x0, blocking collectives: 81.3 us -> none  [by_axis(): return functools.reduce(lax.psum, axes, value)]
    dot_general x7 -> x0, matrix products: 54.5 us -> none  [the longest x2 38.6 us: body(): jnp.dot(error, snaps.reshape(snaps.shape[0], -1), precision=lax.Precision...]
    all_to_all x0 -> x2, blocking collectives: none -> 32.3 us  [exchange(): return lax.all_to_all(value, axes, split_axis=0, concat_axis=0, tiled=True)]
    unnamed x32 -> x13, local copies, waits for them, and re-layouts: 27.8 us -> 0.65 us
    pallas_call x0 -> x6, Pallas kernels: none -> 26.3 us  [call(): run(*[at_home(x, spec) for x, spec in zip(args, specs)])]
    slice x6 -> x2, local copies, waits for them, and re-layouts: 18.2 us -> 0.01 us  [body(): corners = jnp.concatenate([from_up[0:40], from_down[0:40]], axis=1)]
    ppermute x4 -> x0, local copies, waits for them, and re-layouts: 12.5 us -> none  [the longest x2 6.29 us: extended(): lax.ppermute(leading, axis, [(b, a) for a, b in up])]
    ppermute x8 -> x4, starting transfers between devices: 19 us -> 10.2 us  [moved(): lax.ppermute(value, axes, pairs if ahead else [(b, a) for a, b in pairs])]
  transfers between devices with their start and end apart: 8 -> 4, of which waited for: 0 -> 0; matrix products, arithmetic and copies ran while one was open for 24% -> 0% of each run, Pallas kernels for 0% -> 15%
where the time goes in v1:
time: 70.6 us; the launch traced here: 70.3 us
  blocking collectives  32.3 us (46%)
  Pallas kernels  26.3 us (37%)
  starting transfers between devices  10.2 us (14%)
  between operations  0.8 us (1%)
    all_to_all x2, blocking collectives, exchange(): return lax.all_to_all(value, axes, split_axis=0, concat_axis=0, tiled=True)  32.3 us
    pallas_call x6, Pallas kernels, call(): run(*[at_home(x, spec) for x, spec in zip(args, specs)])  26.3 us
    ppermute x4, starting transfers between devices, moved(): lax.ppermute(value, axes, pairs if ahead else [(b, a) for a, b in pairs])  10.2 us
  transfers between devices with their start and end apart: 4, of which 0 were waited for; matrix products, arithmetic and copies ran while one was open for 0% of the time, Pallas kernels for 15%

profile of v1, /device:TPU:32, one launch (start us, length us, event | category | flops | bytes accessed | tf_op | source)
XLA Modules:
  0.0 70.3 jit_solution(7278287542543732753)
XLA Ops:
  0.6 1.1 %line_ends.1 = (f32[96,128]{1,0:T(8,128)S(1)}, f32[96,128]{1,0:T(8,128)S(1)}) custom-call(f32[40,256,128]{2,1,0:T(8,128)} %w_hbm.3, f32[12,256,128]{2,1,0:T(8,128)} %pool_hbm.3), custom_call_target="tpu_custom_call" | custom-call | tf_op jit(solution)/shard_map/line_ends/pallas_call | solution.py:352
  1.8 1.3 %collective-permute-start.1 = (f32[96,128]{1,0:T(8,128)S(1)}, f32[96,128]{1,0:T(8,128)S(1)}, u32[]{:S(2)}, u32[]{:S(2)}) collective-permute-start(f32[96,128]{1,0:T(8,128)S(1)} %get-tuple-element.19.top_ref), channel_id=1, source_target_pairs={{32,0},{64,32},{96,64},{128,96},{160,128},{192,160},{224,192},{33,... | collective-permute-start | bytes 147464 | tf_op jit(solution)/shard_map/ppermute | solution.py:366
  3.0 3.0 %collective-permute-start = (f32[96,128]{1,0:T(8,128)S(1)}, f32[96,128]{1,0:T(8,128)S(1)}, u32[]{:S(2)}, u32[]{:S(2)}) collective-permute-start(f32[96,128]{1,0:T(8,128)S(1)} %get-tuple-element.20.bottom_ref), channel_id=1, source_target_pairs={{0,32},{32,64},{64,96},{96,128},{128,160},{160,192},{192,224},{1,3... | collective-permute-start | bytes 147464 | tf_op jit(solution)/shard_map/ppermute | solution.py:366
  6.1 4.9 %column_ends.1 = (f32[96,256]{1,0:T(8,128)S(1)}, f32[96,256]{1,0:T(8,128)S(1)}, f32[40,256,128]{2,1,0:T(8,128)S(1)}, f32[12,256,128]{2,1,0:T(8,128)S(1)}) custom-call(f32[40,256,128]{2,1,0:T(8,128)} %w_hbm.3, f32[12,256,128]{2,1,0:T(8,128)} %pool_hbm.3), custom_call_target="tpu_custom_call" | custom-call | tf_op jit(solution)/shard_map/column_ends/pallas_call | solution.py:352
  10.9 0.0 copy-start
  11.0 0.0 copy-start.1
  11.0 0.0 collective-permute-done.1.down_ref
  11.0 0.0 collective-permute-done.up_ref
  11.0 3.7 %collective-permute-start.3 = (f32[136,256]{1,0:T(8,128)S(1)}, f32[136,256]{1,0:T(8,128)S(1)}, u32[]{:S(2)}, u32[]{:S(2)}) collective-permute-start(f32[136,256]{1,0:T(8,128)S(1)} %get-tuple-element.28), channel_id=1, source_target_pairs={{1,0},{2,1},{3,2},{4,3},{5,4},{6,5},{7,6},{8,7},{9,8},{10,9},{11,1... | collective-permute-start | bytes 417800 | tf_op jit(solution)/shard_map/ppermute | solution.py:366
  14.8 2.1 %collective-permute-start.2 = (f32[136,256]{1,0:T(8,128)S(1)}, f32[136,256]{1,0:T(8,128)S(1)}, u32[]{:S(2)}, u32[]{:S(2)}) collective-permute-start(f32[136,256]{1,0:T(8,128)S(1)} %get-tuple-element.29), channel_id=1, source_target_pairs={{0,1},{1,2},{2,3},{3,4},{4,5},{5,6},{6,7},{7,8},{8,9},{9,10},{10,1... | collective-permute-start | bytes 417800 | tf_op jit(solution)/shard_map/ppermute | solution.py:366
  16.9 5.8 %gram.1 = (f32[12,128]{1,0:T(8,128)S(1)}, f32[12,256,128]{2,1,0:T(8,128)S(1)}) custom-call(f32[40,256,128]{2,1,0:T(8,128)S(1)} %get-tuple-element.15.w_ref, f32[12,256,128]{2,1,0:T(8,128)S(1)} %get-tuple-element.16.pool_ref), custom_call_target="tpu_custom_call" | custom-call | tf_op jit(solution)/shard_map/gram/pallas_call | solution.py:352
  22.7 0.0 copy-start.2
  22.7 0.0 copy-start.3
  22.7 0.0 copy-start.4
  22.7 0.0 copy-start.5
  22.7 0.0 collective-permute-done.3.east_ref
  22.7 0.0 collective-permute-done.2.west_ref
  22.7 0.0 copy-done
  22.7 0.0 copy-done.1
  22.7 9.0 %base.1 = (f32[16,12,128]{2,1,0:T(8,128)S(1)}, f32[40,256,128]{2,1,0:T(8,128)S(1)}, f32[12,256,128]{2,1,0:T(8,128)S(1)}) custom-call(f32[40]{0:T(128)S(1)} %copy-done, s32[40]{0:T(128)S(1)} %copy-done.1, f32[40,256,128]{2,1,0:T(8,128)S(1)} %get-tuple-element.15.w_ref, f32[12,256,128]{2,1,0:T(8,128)S(1)} %get-tuple-element.17.pool_lap_ref, ...), custom_call_target="tpu_custom_call" | custom-call | tf_op jit(solution)/shard_map/base/pallas_call | solution.py:352
  31.8 17.6 %all_to_all.10.parts_ref = f32[16,12,128]{2,1,0:T(8,128)S(1)} all-to-all(f32[16,12,128]{2,1,0:T(8,128)S(1)} %get-tuple-element.23), channel_id=1, replica_groups=mesh['row_0'=4,'row_1'=2,'col_0'=4,'col_1'=8] {'row_1','col_1'}, dimensions={0} | all-to-all | bytes 196608 | tf_op jit(solution)/shard_map/all_to_all | solution.py:370
  49.4 14.7 %all_to_all.11.parts_ref = f32[16,12,128]{2,1,0:T(8,128)S(1)} all-to-all(f32[16,12,128]{2,1,0:T(8,128)S(1)} %again.1), channel_id=1, replica_groups=mesh['row_0'=4,'row_1'=2,'col_0'=4,'col_1'=8] {'row_0','col_0'}, dimensions={0} | all-to-all | bytes 196608 | tf_op jit(solution)/shard_map/all_to_all | solution.py:370
  64.1 0.0 copy-done.2
  64.1 0.0 copy-done.3
  64.1 0.0 copy-done.4
  64.1 0.0 copy-done.5
  64.1 5.6 %finish.1 = (f32[40,256,128]{2,1,0:T(8,128)}, f32[2,16,40]{2,1,0:T(8,128)S(1)}) custom-call(f32[16,12,128]{2,1,0:T(8,128)S(1)} %all_to_all.11.parts_ref, f32[8,12]{1,0:T(8,128)S(1)} %bitcast.11, s32[2,16]{1,0:T(2,128)S(1)} %copy-done.3, s32[1,40]{1,0:T(1,128)S(1)} %bitcast.12, f32[1,40]{1,0:T(1,128)S(1)} %bitcast.13, f32[1,40]{1,0:T(1,128)S(1)} %bitcast.8, ...), custom_call_target="tpu_custom_call" | custom-call | tf_op jit(solution)/shard_map/finish/pallas_call | solution.py:352
  69.7 0.6 copy.10
  (4 shorter events, 0.1 us)
Async XLA Ops:
  1.8 9.2 %collective-permute-start.1 = (f32[96,128]{1,0:T(8,128)S(1)}, f32[96,128]{1,0:T(8,128)S(1)}, u32[]{:S(2)}, u32[]{:S(2)}) collective-permute-start(f32[96,128]{1,0:T(8,128)S(1)} %get-tuple-element.19.top_ref), channel_id=1, source_target_pairs={{32,0},{64,32},{96,64},{128,96},{160,128},{192,160},{224,192},{33,... | collective-permute-start | bytes 147464 | tf_op jit(solution)/shard_map/ppermute | solution.py:366
  3.0 7.9 %collective-permute-start = (f32[96,128]{1,0:T(8,128)S(1)}, f32[96,128]{1,0:T(8,128)S(1)}, u32[]{:S(2)}, u32[]{:S(2)}) collective-permute-start(f32[96,128]{1,0:T(8,128)S(1)} %get-tuple-element.20.bottom_ref), channel_id=1, source_target_pairs={{0,32},{32,64},{64,96},{96,128},{128,160},{160,192},{192,224},{1,3... | collective-permute-start | bytes 147464 | tf_op jit(solution)/shard_map/ppermute | solution.py:366
  10.9 11.8 %copy-start = (f32[40]{0:T(128)S(1)}, f32[40]{0:T(128)}, u32[]{:S(2)}) copy-start(f32[40]{0:T(128)} %smooth_ref.1) | copy-start | bytes 484
  11.0 11.8 %copy-start.1 = (s32[40]{0:T(128)S(1)}, s32[40]{0:T(128)}, u32[]{:S(2)}) copy-start(s32[40]{0:T(128)} %active_ref.1) | copy-start | bytes 484
  11.0 11.7 %collective-permute-start.3 = (f32[136,256]{1,0:T(8,128)S(1)}, f32[136,256]{1,0:T(8,128)S(1)}, u32[]{:S(2)}, u32[]{:S(2)}) collective-permute-start(f32[136,256]{1,0:T(8,128)S(1)} %get-tuple-element.28), channel_id=1, source_target_pairs={{1,0},{2,1},{3,2},{4,3},{5,4},{6,5},{7,6},{8,7},{9,8},{10,9},{11,1... | collective-permute-start | bytes 417800 | tf_op jit(solution)/shard_map/ppermute | solution.py:366
  14.8 7.9 %collective-permute-start.2 = (f32[136,256]{1,0:T(8,128)S(1)}, f32[136,256]{1,0:T(8,128)S(1)}, u32[]{:S(2)}, u32[]{:S(2)}) collective-permute-start(f32[136,256]{1,0:T(8,128)S(1)} %get-tuple-element.29), channel_id=1, source_target_pairs={{0,1},{1,2},{2,3},{3,4},{4,5},{5,6},{6,7},{7,8},{8,9},{9,10},{10,1... | collective-permute-start | bytes 417800 | tf_op jit(solution)/shard_map/ppermute | solution.py:366
  22.7 41.4 %copy-start.2 = (f32[12,8]{0,1:T(8,128)S(1)}, f32[12,8]{0,1:T(8,128)}, u32[]{:S(2)}) copy-start(f32[12,8]{0,1:T(8,128)} %param.10) | copy-start | bytes 1156
  22.7 41.4 %copy-start.3 = (s32[2,16]{1,0:T(2,128)S(1)}, s32[2,16]{1,0:T(2,128)}, u32[]{:S(2)}) copy-start(s32[2,16]{1,0:T(2,128)} %plan_ref.1) | copy-start | bytes 388
  22.7 41.4 %copy-start.4 = (s32[40]{0:T(128)S(1)}, s32[40]{0:T(128)}, u32[]{:S(2)}) copy-start(s32[40]{0:T(128)} %param.12) | copy-start | bytes 484
  22.7 41.4 %copy-start.5 = (f32[40]{0:T(128)S(1)}, f32[40]{0:T(128)}, u32[]{:S(2)}) copy-start(f32[40]{0:T(128)} %param.13) | copy-start | bytes 484

commit v2 on v1

--- a/solution.py
+++ b/solution.py
@@ -66,11 +66,11 @@
     return jnp.where(away == 0, center, jnp.where(away == 1, 1.0, 0.0))
 
 
-def lap_inside(x, along):
-    return rows_around(x) + dot(jnp.concatenate(halves(x), axis=1), along, NN)
-
-
-def line_ends(w_hbm, pool_hbm, top_ref, bottom_ref, w_buf, pool_buf, sems):
+def by_side(even, first, second):
+    return jnp.where(even, second, first), jnp.where(even, first, second)
+
+
+def line_ends(w_hbm, pool_hbm, first_ref, second_ref, w_buf, pool_buf, sems):
     copies = []
     for k, at in enumerate((0, ROWS - 8)):
         for j, (src, dst) in enumerate(((w_hbm, w_buf), (pool_hbm, pool_buf))):
@@ -79,18 +79,20 @@
         copy.start()
     for copy in copies:
         copy.wait()
-    for k, (ref, near, far) in enumerate(((top_ref, 0, 1), (bottom_ref, 7, 6))):
-        ref[0:40, :] = w_buf[k, :, near, :]
-        ref[40:80, :] = w_buf[k, :, far, :]
-        ref[80:96, :] = jnp.zeros((16, LANES), F32)
-        ref[80:92, :] = pool_buf[k, :, near, :]
-
-
-def column_ends(w_hbm, pool_hbm, left_ref, right_ref, w_buf, pool_buf, ends_ref, sems):
+    even = lax.axis_index(ROW[1]) == 0
+    for rows, buf, top, bottom in (
+        (slice(0, 40), w_buf, 0, 7), (slice(40, 80), w_buf, 1, 6), (slice(80, 92), pool_buf, 0, 7)
+    ):
+        first_ref[rows, :], second_ref[rows, :] = by_side(even, buf[0, :, top, :], buf[1, :, bottom, :])
+    for ref in (first_ref, second_ref):
+        ref[92:96, :] = jnp.zeros((4, LANES), F32)
+
+
+def column_ends(w_hbm, pool_hbm, first_ref, second_ref, w_buf, pool_buf, lap_ref, ends_ref, sems):
     copies = [pltpu.make_async_copy(pool_hbm, pool_buf, sems.at[5])]
     for k in range(5):
         copies.append(pltpu.make_async_copy(w_hbm.at[8 * k : 8 * k + 8], w_buf.at[8 * k : 8 * k + 8], sems.at[k]))
-    for copy in copies:
+    for copy in copies[:2]:
         copy.start()
     row, lane = iota((8, LANES), 0), iota((8, LANES), 1)
     pick = jnp.zeros((8, LANES), F32)
@@ -98,36 +100,41 @@
         pick = jnp.where((row == k) & (lane == spot), 1.0, pick)
     pick = pick.astype(BF16)
     pick = jnp.concatenate([pick, pick], axis=1)
-
-    def taken(ref, first):
-        def image(p, carry):
-            ends_ref[first + p] = dot(pick, jnp.concatenate(halves(ref[p]), axis=1), NT)
-            return carry
-
-        return image
-
-    copies[0].wait()
-    lax.fori_loop(0, POOL, taken(pool_buf, BEAMS), 0, unroll=4)
-    for k in range(5):
-        copies[1 + k].wait()
-        lax.fori_loop(8 * k, 8 * k + 8, taken(w_buf, 0), 0, unroll=4)
-    for ref, near, far in ((left_ref, 0, 2), (right_ref, 1, 3)):
-        ref[0:40, :] = ends_ref[0:40, near, :]
-        ref[40:80, :] = ends_ref[0:40, far, :]
-        ref[80:96, :] = jnp.zeros((16, ROWS), F32)
-        ref[80:92, :] = ends_ref[40:52, near, :]
-
-
-def gram(w_ref, pool_ref, sums_ref, lap_ref, acc_ref):
     along = band_matrix(-4.0).astype(BF16)
     along = jnp.concatenate([along, along], axis=0)
+
+    def image(p, carry):
+        x = pool_buf[p]
+        both = jnp.concatenate(halves(x), axis=1)
+        ends_ref[BEAMS + p] = dot(pick, both, NT)
+        lap_ref[p] = rows_around(x) + dot(both, along, NN)
+        return carry
+
+    def beam(b, carry):
+        ends_ref[b] = dot(pick, jnp.concatenate(halves(w_buf[b]), axis=1), NT)
+        return carry
+
+    for k, copy in enumerate(copies):
+        copy.wait()
+        if k == 0:
+            copies[2].start()
+            copies[3].start()
+            lax.fori_loop(0, POOL, image, 0, unroll=4)
+        else:
+            if k + 3 < len(copies):
+                copies[k + 3].start()
+            lax.fori_loop(8 * k - 8, 8 * k, beam, 0, unroll=4)
+    even = (lax.axis_index(COL[1]) & 1) == 0
+    for rows, images, left, right in (
+        (slice(0, 40), slice(0, 40), 0, 1), (slice(40, 80), slice(0, 40), 2, 3), (slice(80, 92), slice(40, 52), 0, 1)
+    ):
+        first_ref[rows, :], second_ref[rows, :] = by_side(even, ends_ref[images, left, :], ends_ref[images, right, :])
+    for ref in (first_ref, second_ref):
+        ref[92:96, :] = jnp.zeros((4, ROWS), F32)
+
+
+def gram(w_ref, pool_ref, lap_ref, sums_ref, acc_ref):
     acc_ref[...] = jnp.zeros_like(acc_ref)
-
-    def smooth(p, carry):
-        lap_ref[p] = lap_inside(pool_ref[p], along)
-        return carry
-
-    lax.fori_loop(0, POOL, smooth, 0, unroll=4)
 
     def pair(ref, count, t):
         parts = []
@@ -173,9 +180,19 @@
 
 def base(
     smooth_ref, active_ref, w_ref, pool_lap_ref, sums_ref, smooth_row_ref, active_row_ref,
-    top_ref, bottom_ref, left_ref, right_ref, up_ref, down_ref, west_ref, east_ref,
-    sent_ref, out_ref, lap_ref, fix_ref, p_fix_ref,
+    row_a, row_b, row_a_got, row_b_got, col_a, col_b, col_a_got, col_b_got,
+    sent_ref, out_ref, lap_ref, fix_ref, turned_ref, slots_ref,
+    top_ref, bottom_ref, up_ref, down_ref, left_ref, right_ref, west_ref, east_ref,
 ):
+    even_row = lax.axis_index(ROW[1]) == 0
+    even_col = (lax.axis_index(COL[1]) & 1) == 0
+    top_ref[...], bottom_ref[...] = by_side(even_row, row_a[...], row_b[...])
+    up_ref[...], down_ref[...] = by_side(even_row, row_a_got[...], row_b_got[...])
+    left_ref[...], right_ref[...] = by_side(even_col, col_a[...], col_b[...])
+    west_ref[...], east_ref[...] = by_side(even_col, col_a_got[...], col_b_got[...])
+    for ref in (west_ref, east_ref):
+        one, two = ref[96:136, 0:LANES], ref[96:136, LANES:]
+        ref[96:136, 0:LANES], ref[96:136, LANES:] = by_side(even_row, one, two)
     halo = jnp.concatenate([ref[80:96, :] for ref in (west_ref, east_ref, up_ref, down_ref)], axis=1)
     edge = jnp.concatenate([ref[0:40, :] for ref in (left_ref, right_ref, top_ref, bottom_ref)], axis=1)
     edge = jnp.concatenate([jnp.zeros((40, 768), F32), edge, jnp.zeros((48, 768), F32)], axis=0)
@@ -201,67 +218,83 @@
     def mixed(near, far, own, prev, after):
         return a * near + c * (2.0 * (prev + after) - 8.0 * near + far + own), c * near
 
-    def column(msg_ref, own_ref, has):
-        near = msg_ref[span, :]
+    def column(msg_ref, own_ref, far_ref, has):
+        near = msg_ref[span, :] - far_ref[span, :]
         prev = jnp.where(wide == 0, 0.0, pltpu.roll(near, 1, 1))
         after = jnp.where(wide == ROWS - 1, 0.0, pltpu.roll(near, ROWS - 1, 1))
-        return mixed(near, msg_ref[shifted, :], has * own_ref[span, :], prev, after)
-
-    def line(msg_ref, own_ref, has, at):
-        near = msg_ref[span, :]
-        west = pltpu.roll(west_ref[corner, at : at + LANES], 1, 1)
-        east = pltpu.roll(east_ref[corner, at : at + LANES], LANES - 1, 1)
+        far = msg_ref[shifted, :] - far_ref[shifted, :]
+        return mixed(near, far, (has - 1.0) * own_ref[span, :], prev, after)
+
+    def line(msg_ref, own_ref, far_ref, has, at):
+        near = msg_ref[span, :] - far_ref[span, :]
+        west = pltpu.roll(west_ref[corner, at : at + LANES] - far_ref[span, :], 1, 1)
+        east = pltpu.roll(east_ref[corner, at : at + LANES] - far_ref[span, :], LANES - 1, 1)
         prev = jnp.where(thin == 0, west, pltpu.roll(near, 1, 1))
         after = jnp.where(thin == LANES - 1, east, pltpu.roll(near, LANES - 1, 1))
-        return mixed(near, msg_ref[shifted, :], has * own_ref[span, :], prev, after)
+        far = msg_ref[shifted, :] - far_ref[shifted, :]
+        return mixed(near, far, (has - 1.0) * own_ref[span, :], prev, after)
 
     fix_ref[...] = jnp.zeros_like(fix_ref)
-    fix_ref[:, 0, 0:256], fix_ref[:, 1, 0:256] = column(west_ref, left_ref, has_west)
-    fix_ref[:, 2, 0:256], fix_ref[:, 3, 0:256] = column(east_ref, right_ref, has_east)
-    fix_ref[:, 0, 256:384], fix_ref[:, 1, 256:384] = line(up_ref, top_ref, has_up, 0)
-    fix_ref[:, 7, 384:512], fix_ref[:, 6, 384:512] = line(down_ref, bottom_ref, has_down, LANES)
-
-    row, lane = iota((16, LANES), 0) & 7, iota((16, LANES), 1)
-    place = jnp.zeros((16, LANES), F32)
-    for k, spot in enumerate((0, 1, LANES - 1, LANES - 2)):
-        place = jnp.where((row == k) & (lane == spot), 1.0, place)
-    place = place.astype(BF16)
-
-    def placed(x):
-        high, low = halves(x)
-        both = jnp.concatenate([high.astype(F32), low.astype(F32)], axis=0)
-        return dot(both.T.astype(BF16), place, NN)
-
-    p_fix_ref[...] = jnp.zeros_like(p_fix_ref)
-    p_fix_ref[:, 0, :] = west_ref[80:92, :]
-    p_fix_ref[:, 2, :] = east_ref[80:92, :]
+    turned_ref[...] = jnp.zeros_like(turned_ref)
+
+    def beams_at(k):
+        return pl.ds(k, BEAMS, stride=4)
+
+    def pools_at(k):
+        return pl.ds(4 * BEAMS + k, POOL, stride=4)
+
+    east, west = column(east_ref, right_ref, left_ref, has_east), column(west_ref, left_ref, right_ref, has_west)
+    for k, (line_of, pool_of) in enumerate(
+        ((east[1], None), (east[0], east_ref[80:92, :]), (west[0], west_ref[80:92, :]), (west[1], None))
+    ):
+        for h in range(2):
+            part = slice(LANES * h, LANES * (h + 1))
+            turned_ref[h, beams_at(k), :] = line_of[:, part]
+            if pool_of is not None:
+                turned_ref[h, pools_at(k), :] = pool_of[:, part]
+    for k in range(2):
+        for h in range(2):
+            part = slice(LANES * h, LANES * (h + 1))
+            slots_ref[k, part, :] = turned_ref[h, LANES * k : LANES * (k + 1), :].T
+    fix_ref[:, 0, 0:128], fix_ref[:, 1, 0:128] = line(up_ref, top_ref, bottom_ref, has_up, 0)
+    fix_ref[:, 7, 128:256], fix_ref[:, 6, 128:256] = line(down_ref, bottom_ref, top_ref, has_down, LANES)
+    lane = iota((ROWS, LANES), 1)
+    at_edge = (lane < 2) | (lane >= LANES - 2)
+
+    def placed(image):
+        spun = pltpu.roll(slots_ref[image >> 5], (LANES - 2 - 4 * image) & (LANES - 1), 1)
+        return jnp.where(at_edge, spun, 0.0)
 
     def pool_step(p, carry):
-        lap_ref[p] = pool_lap_ref[p] + placed(p_fix_ref[p])
+        lap_ref[p] = pool_lap_ref[p] + placed(BEAMS + p)
         return carry
 
     lax.fori_loop(0, POOL, pool_step, 0, unroll=4)
     lap_ref[:, 0, :] += up_ref[80:92, :]
     lap_ref[:, ROWS - 1, :] += down_ref[80:92, :]
 
-    once = band_matrix(-2.0)
-    twice = dot(once, once, NN)
-    along = jnp.concatenate([once, twice], axis=1).astype(BF16)
+    away = (iota((LANES, LANES), 0) - iota((LANES, LANES), 1)) & (LANES - 1)
+    once = jnp.where(away == 0, -2.0, jnp.where((away == 1) | (away == LANES - 1), 1.0, 0.0))
+    along = jnp.concatenate([once, dot(once, once, NN)], axis=1).astype(BF16)
     along = jnp.concatenate([along, along], axis=0)
 
+    def around(x):
+        return pltpu.roll(x, 1, 0) + pltpu.roll(x, ROWS - 1, 0)
+
     def beam(b, carry):
+        s_b, n_b = smooth_ref[b], active_ref[b]
+        r_0, r_1 = jnp.where(n_b > 0, s_b, 0.0), jnp.where(n_b > 1, s_b, 0.0)
+        a_b, c_b = r_0 + r_1, r_0 * r_1
         x = w_ref[b]
-        s_b, n_b = smooth_ref[b], active_ref[b]
-        live0, live1 = jnp.where(n_b > 0, 1.0, 0.0), jnp.where(n_b > 1, 1.0, 0.0)
-        a_b, c_b = s_b * (live0 + live1), s_b * s_b * live0 * live1
         sides = dot(jnp.concatenate(halves(x), axis=1), along, NN)
         one, two = sides[:, :LANES], sides[:, LANES:]
-        down = rows_around(x) - 2.0 * x
-        inner = a_b * x + c_b * (down + 2.0 * one)
-        out = (x + a_b * one + c_b * two) + (rows_around(inner) - 2.0 * inner) + placed(fix_ref[b, :, 0:256])
+        lines = around(x)
+        inner = around((a_b - 2.0 * c_b) * x + (2.0 * c_b) * one + c_b * lines)
+        kept = (1.0 - 2.0 * a_b + 4.0 * c_b) * x + (a_b - 4.0 * c_b) * one + c_b * two - (2.0 * c_b) * lines
+        out = kept + inner + placed(b)
         out_ref[b, 8 : ROWS - 8, :] = out[8 : ROWS - 8]
-        out_ref[b, 0:8, :] = out[0:8] + fix_ref[b, :, 256:384]
-        out_ref[b, ROWS - 8 : ROWS, :] = out[ROWS - 8 :] + fix_ref[b, :, 384:512]
+        out_ref[b, 0:8, :] = out[0:8] + fix_ref[b, :, 0:128]
+        out_ref[b, ROWS - 8 : ROWS, :] = out[ROWS - 8 :] + fix_ref[b, :, 128:256]
         return carry
 
     lax.fori_loop(0, BEAMS, beam, 0, unroll=2)
@@ -300,14 +333,13 @@
     gap = jnp.zeros((4, BEAMS), F32)
     both = jnp.concatenate([d0, gap, d1, gap], axis=0)
     spread = jnp.where((iota((320, BEAMS), 0) >> 3) == iota((320, BEAMS), 1), 1.0, 0.0)
-    by_q = dot(spread, both, NT, EXACT)
+    spread = spread.astype(BF16)
     q, j = iota((32, 192), 0), iota((32, 192), 1) >> 3
-    fold = jnp.where(((j < POOL) & (q == j)) | ((j >= POOL) & (q == j + 16 - POOL)), 1.0, 0.0)
-    wide = dot(by_q, fold, NN, EXACT)
-    same = (iota(wide.shape, 0) & 7) == (iota(wide.shape, 1) & 7)
-    high, low = halves(jnp.where(same, wide, 0.0))
-    high_ref[...] = high
-    low_ref[...] = low
+    fold = jnp.where(((j < POOL) & (q == j)) | ((j >= POOL) & (q == j + 16 - POOL)), 1.0, 0.0).astype(BF16)
+    same = (iota((320, 192), 0) & 7) == (iota((320, 192), 1) & 7)
+    for ref, part in zip((high_ref, low_ref), halves(both)):
+        by_q = dot(spread, part, NT).astype(BF16)
+        ref[...] = jnp.where(same, dot(by_q, fold, NN), 0.0).astype(BF16)
 
     def step(t, carry):
         def tile(ref, at):
@@ -360,10 +392,10 @@
     return pltpu.HBM(dims, F32)
 
 
-def moved(value, axes, ahead):
+def swapped(value, axes, phase):
     count = lax.axis_size(axes)
-    pairs = [(i, i + 1) for i in range(count - 1)]
-    return lax.ppermute(value, axes, pairs if ahead else [(b, a) for a, b in pairs])
+    pairs = [(i, i + 1) for i in range(phase, count - 1, 2)]
+    return lax.ppermute(value, axes, pairs + [(b, a) for a, b in pairs])
 
 
 def exchange(value, axes):
@@ -372,42 +404,41 @@
 
 def body(weights, pool, desired, plan, beam_ref, step_size, smoothing, active):
     DMA = pltpu.SemaphoreType.DMA
-    top, bottom = call(
+    row_a, row_b = call(
         line_ends,
         [vmem(96, LANES)] * 2,
         [HBM, HBM],
         [vmem(2, BEAMS, 8, LANES), vmem(2, POOL, 8, LANES), DMA((4,))],
     )(weights, pool)
-    from_up = moved(bottom, ROW, True)
-    from_down = moved(top, ROW, False)
-    left, right, w_near, p_near = call(
+    row_b_got = swapped(row_b, ROW, 1)
+    row_a_got = swapped(row_a, ROW, 0)
+    col_a, col_b, w_near, p_near, pool_lap = call(
         column_ends,
-        [vmem(96, ROWS)] * 2 + [vmem(BEAMS, ROWS, LANES), vmem(POOL, ROWS, LANES)],
+        [vmem(96, ROWS)] * 2 + [vmem(BEAMS, ROWS, LANES), vmem(POOL, ROWS, LANES), vmem(POOL, ROWS, LANES)],
         [HBM, HBM],
         [vmem(BEAMS + POOL, 8, ROWS), DMA((6,))],
     )(weights, pool)
-    corners = jnp.concatenate([from_up[0:40], from_down[0:40]], axis=1)
-    from_west = moved(jnp.concatenate([right, corners], axis=0), COL, True)
-    from_east = moved(jnp.concatenate([left, corners], axis=0), COL, False)
-    sums, pool_lap = call(
-        gram, [vmem(POOL, LANES), vmem(POOL, ROWS, LANES)], [VMEM, VMEM], [vmem(416, 192)]
-    )(w_near, p_near)
+    corners = jnp.concatenate([row_a_got[0:40], row_b_got[0:40]], axis=1)
+    col_a_got = swapped(jnp.concatenate([col_a, corners], axis=0), COL, 0)
+    col_b_got = swapped(jnp.concatenate([col_b, corners], axis=0), COL, 1)
+    (sums,) = call(gram, [vmem(POOL, LANES)], [VMEM] * 3, [vmem(416, 192)])(w_near, p_near, pool_lap)
     rows = (smoothing[None, :], active[None, :])
     sent, based, lap = call(
         base,
         [vmem(16, POOL, LANES), vmem(BEAMS, ROWS, LANES), vmem(POOL, ROWS, LANES)],
         [SMEM, SMEM] + [VMEM] * 13,
-        [vmem(BEAMS, 8, 512), vmem(POOL, 8, ROWS)],
+        [vmem(BEAMS, 8, 256), vmem(2, 256, LANES), vmem(2, ROWS, LANES)]
+        + [vmem(96, LANES)] * 4 + [vmem(96, ROWS)] * 2 + [vmem(136, ROWS)] * 2,
     )(
         smoothing, active, w_near, pool_lap, sums, *rows,
-        top, bottom, left, right, from_up, from_down, from_west, from_east,
+        row_a, row_b, row_a_got, row_b_got, col_a, col_b, col_a_got, col_b_got,
     )
     near = exchange(sent, NEAR)
     (sent,) = call(again, [vmem(16, POOL, LANES)], [VMEM])(near)
     far = exchange(sent, FAR)
     final, errors = call(
         finish,
-        [far_out(BEAMS, ROWS, LANES), vmem(2, 16, BEAMS)],
+        [far_out(BEAMS, ROWS, LANES), jax.ShapeDtypeStruct((2, 16, BEAMS), F32)],
         [VMEM] * 10,
         [
             vmem(BEAMS, ROWS, LANES),

time: 70.6 us -> 65.6 us (0.929)
  starting transfers between devices: 10.2 us -> 4.67 us
  blocking collectives: 32.3 us -> 33.8 us
    ppermute x4, starting transfers between devices: 10.2 us -> 4.67 us  [swapped(): return lax.ppermute(value, axes, pairs + [(b, a) for a, b in pairs])]
    all_to_all x2, blocking collectives: 32.3 us -> 33.8 us  [exchange(): return lax.all_to_all(value, axes, split_axis=0, concat_axis=0, tiled=True)]
  transfers between devices with their start and end apart: 4 -> 4, of which waited for: 0 -> 1; matrix products, arithmetic and copies ran while one was open for 0% -> 0% of each run, Pallas kernels for 15% -> 15%
where the time goes in v2:
time: 65.6 us; the launch traced here: 65.3 us
  blocking collectives  33.8 us (52%)
  Pallas kernels  25.9 us (39%)
  starting transfers between devices  4.67 us (7%)
  between operations  0.77 us (1%)
    all_to_all x2, blocking collectives, exchange(): return lax.all_to_all(value, axes, split_axis=0, concat_axis=0, tiled=True)  33.8 us
    pallas_call x6, Pallas kernels, call(): run(*[at_home(x, spec) for x, spec in zip(args, specs)])  25.9 us
    ppermute x4, starting transfers between devices, swapped(): return lax.ppermute(value, axes, pairs + [(b, a) for a, b in pairs])  4.67 us
  transfers between devices with their start and end apart: 4, of which 1 were waited for; matrix products, arithmetic and copies ran while one was open for 0% of the time, Pallas kernels for 15%

profile of v2, /device:TPU:32, one launch (start us, length us, event | category | flops | bytes accessed | tf_op | source)
XLA Modules:
  0.0 65.3 jit_solution(17259538015037073939)
XLA Ops:
  0.6 1.1 %line_ends.1 = (f32[96,128]{1,0:T(8,128)S(1)}, f32[96,128]{1,0:T(8,128)S(1)}) custom-call(f32[40,256,128]{2,1,0:T(8,128)} %w_hbm.3, f32[12,256,128]{2,1,0:T(8,128)} %pool_hbm.3), custom_call_target="tpu_custom_call" | custom-call | tf_op jit(solution)/shard_map/line_ends/pallas_call | solution.py:384
  1.8 0.1 collective-permute-start
  1.9 0.7 %collective-permute-start.1 = (f32[96,128]{1,0:T(8,128)S(1)}, f32[96,128]{1,0:T(8,128)S(1)}, u32[]{:S(2)}, u32[]{:S(2)}) collective-permute-start(f32[96,128]{1,0:T(8,128)S(1)} %get-tuple-element.18.row_b), channel_id=1, source_target_pairs={{32,64},{96,128},{160,192},{64,32},{128,96},{192,160},{33,65},{97,... | collective-permute-start | bytes 147464 | tf_op jit(solution)/shard_map/ppermute | solution.py:398
  2.6 5.2 %column_ends.1 = (f32[96,256]{1,0:T(8,128)S(1)}, f32[96,256]{1,0:T(8,128)S(1)}, f32[40,256,128]{2,1,0:T(8,128)S(1)}, f32[12,256,128]{2,1,0:T(8,128)S(1)}, f32[12,256,128]{2,1,0:T(8,128)S(1)}) custom-call(f32[40,256,128]{2,1,0:T(8,128)} %w_hbm.3, f32[12,256,128]{2,1,0:T(8,128)} %pool_hbm.3), custom_call_target="tpu_custom_call" | custom-call | tf_op jit(solution)/shard_map/column_ends/pallas_call | solution.py:384
  7.7 0.0 copy-start
  7.7 0.0 copy-start.1
  7.8 0.0 collective-permute-done.row_a_got
  7.8 0.0 collective-permute-done.1.row_b_got
  7.8 3.8 %collective-permute-start.3 = (f32[136,256]{1,0:T(8,128)S(1)}, f32[136,256]{1,0:T(8,128)S(1)}, u32[]{:S(2)}, u32[]{:S(2)}) collective-permute-start(f32[136,256]{1,0:T(8,128)S(1)} %get-tuple-element.26), channel_id=1, source_target_pairs={{1,2},{3,4},{5,6},{7,8},{9,10},{11,12},{13,14},{15,16},{17,18},{19... | collective-permute-start | bytes 417800 | tf_op jit(solution)/shard_map/ppermute | solution.py:398
  11.7 0.1 collective-permute-start.2
  11.8 4.8 %gram.1.sums_ref = f32[12,128]{1,0:T(8,128)S(1)} custom-call(f32[40,256,128]{2,1,0:T(8,128)S(1)} %get-tuple-element.14.w_ref, f32[12,256,128]{2,1,0:T(8,128)S(1)} %get-tuple-element.16.pool_ref, f32[12,256,128]{2,1,0:T(8,128)S(1)} %get-tuple-element.15.lap_ref.pool_lap_ref), custom_call_target="tpu_custom_call" | custom-call | tf_op jit(solution)/shard_map/gram/pallas_call | solution.py:384
  16.6 0.0 copy-start.2
  16.6 0.0 copy-start.3
  16.6 0.0 copy-start.4
  16.6 0.0 copy-start.5
  16.6 0.0 collective-permute-done.3.col_b_got
  16.6 0.2 collective-permute-done.2.col_a_got
  16.8 0.0 copy-done
  16.8 0.0 copy-done.1
  16.8 8.9 %base.1 = (f32[16,12,128]{2,1,0:T(8,128)S(1)}, f32[40,256,128]{2,1,0:T(8,128)S(1)}, f32[12,256,128]{2,1,0:T(8,128)S(1)}) custom-call(f32[40]{0:T(128)S(1)} %copy-done, s32[40]{0:T(128)S(1)} %copy-done.1, f32[40,256,128]{2,1,0:T(8,128)S(1)} %get-tuple-element.14.w_ref, f32[12,256,128]{2,1,0:T(8,128)S(1)} %get-tuple-element.15.lap_ref.pool_lap_ref, ...), custom_call_target="tpu_custom_call" | custom-call | tf_op jit(solution)/shard_map/base/pallas_call | solution.py:384
  25.7 18.5 %all_to_all.10.parts_ref = f32[16,12,128]{2,1,0:T(8,128)S(1)} all-to-all(f32[16,12,128]{2,1,0:T(8,128)S(1)} %get-tuple-element.21), channel_id=1, replica_groups=mesh['row_0'=4,'row_1'=2,'col_0'=4,'col_1'=8] {'row_1','col_1'}, dimensions={0} | all-to-all | bytes 196608 | tf_op jit(solution)/shard_map/all_to_all | solution.py:402
  44.3 15.2 %all_to_all.11.parts_ref = f32[16,12,128]{2,1,0:T(8,128)S(1)} all-to-all(f32[16,12,128]{2,1,0:T(8,128)S(1)} %again.1), channel_id=1, replica_groups=mesh['row_0'=4,'row_1'=2,'col_0'=4,'col_1'=8] {'row_0','col_0'}, dimensions={0} | all-to-all | bytes 196608 | tf_op jit(solution)/shard_map/all_to_all | solution.py:402
  59.5 0.0 copy-done.2
  59.5 0.0 copy-done.3
  59.5 0.0 copy-done.4
  59.5 0.0 copy-done.5
  59.5 5.8 %finish.1 = (f32[40,256,128]{2,1,0:T(8,128)}, f32[2,16,40]{2,1,0:T(8,128)}) custom-call(f32[16,12,128]{2,1,0:T(8,128)S(1)} %all_to_all.11.parts_ref, f32[8,12]{1,0:T(8,128)S(1)} %bitcast.10, s32[2,16]{1,0:T(2,128)S(1)} %copy-done.3, s32[1,40]{1,0:T(1,128)S(1)} %bitcast.11, f32[1,40]{1,0:T(1,128)S(1)} %bitcast.12, f32[1,40]{1,0:T(1,128)S(1)} %bitcast.7, ...), custom_call_target="tpu_custom_call" | custom-call | tf_op jit(solution)/shard_map/finish/pallas_call | solution.py:384
  (4 shorter events, 0.1 us)
Async XLA Ops:
  1.8 6.0 %collective-permute-start = (f32[96,128]{1,0:T(8,128)S(1)}, f32[96,128]{1,0:T(8,128)S(1)}, u32[]{:S(2)}, u32[]{:S(2)}) collective-permute-start(f32[96,128]{1,0:T(8,128)S(1)} %get-tuple-element.17.row_a), channel_id=1, source_target_pairs={{0,32},{64,96},{128,160},{192,224},{32,0},{96,64},{160,128},{224,1... | collective-permute-start | bytes 147464 | tf_op jit(solution)/shard_map/ppermute | solution.py:398
  1.9 5.9 %collective-permute-start.1 = (f32[96,128]{1,0:T(8,128)S(1)}, f32[96,128]{1,0:T(8,128)S(1)}, u32[]{:S(2)}, u32[]{:S(2)}) collective-permute-start(f32[96,128]{1,0:T(8,128)S(1)} %get-tuple-element.18.row_b), channel_id=1, source_target_pairs={{32,64},{96,128},{160,192},{64,32},{128,96},{192,160},{33,65},{97,... | collective-permute-start | bytes 147464 | tf_op jit(solution)/shard_map/ppermute | solution.py:398
  7.7 9.1 %copy-start = (f32[40]{0:T(128)S(1)}, f32[40]{0:T(128)}, u32[]{:S(2)}) copy-start(f32[40]{0:T(128)} %smooth_ref.1) | copy-start | bytes 484
  7.7 9.1 %copy-start.1 = (s32[40]{0:T(128)S(1)}, s32[40]{0:T(128)}, u32[]{:S(2)}) copy-start(s32[40]{0:T(128)} %active_ref.1) | copy-start | bytes 484
  7.8 8.8 %collective-permute-start.3 = (f32[136,256]{1,0:T(8,128)S(1)}, f32[136,256]{1,0:T(8,128)S(1)}, u32[]{:S(2)}, u32[]{:S(2)}) collective-permute-start(f32[136,256]{1,0:T(8,128)S(1)} %get-tuple-element.26), channel_id=1, source_target_pairs={{1,2},{3,4},{5,6},{7,8},{9,10},{11,12},{13,14},{15,16},{17,18},{19... | collective-permute-start | bytes 417800 | tf_op jit(solution)/shard_map/ppermute | solution.py:398
  11.7 5.1 %collective-permute-start.2 = (f32[136,256]{1,0:T(8,128)S(1)}, f32[136,256]{1,0:T(8,128)S(1)}, u32[]{:S(2)}, u32[]{:S(2)}) collective-permute-start(f32[136,256]{1,0:T(8,128)S(1)} %get-tuple-element.27), channel_id=1, source_target_pairs={{0,1},{2,3},{4,5},{6,7},{8,9},{10,11},{12,13},{14,15},{16,17},{18,... | collective-permute-start | bytes 417800 | tf_op jit(solution)/shard_map/ppermute | solution.py:398
  16.6 42.9 %copy-start.2 = (f32[12,8]{0,1:T(8,128)S(1)}, f32[12,8]{0,1:T(8,128)}, u32[]{:S(2)}) copy-start(f32[12,8]{0,1:T(8,128)} %param.10) | copy-start | bytes 1156
  16.6 42.9 %copy-start.3 = (s32[2,16]{1,0:T(2,128)S(1)}, s32[2,16]{1,0:T(2,128)}, u32[]{:S(2)}) copy-start(s32[2,16]{1,0:T(2,128)} %plan_ref.1) | copy-start | bytes 388
  16.6 42.9 %copy-start.4 = (s32[40]{0:T(128)S(1)}, s32[40]{0:T(128)}, u32[]{:S(2)}) copy-start(s32[40]{0:T(128)} %param.12) | copy-start | bytes 484
  16.6 42.9 %copy-start.5 = (f32[40]{0:T(128)S(1)}, f32[40]{0:T(128)}, u32[]{:S(2)}) copy-start(f32[40]{0:T(128)} %param.13) | copy-start | bytes 484

commit v3 on v2

--- a/solution.py
+++ b/solution.py
@@ -1,3 +1,4 @@
+import functools
 import math
 
 import jax
@@ -18,6 +19,7 @@
 BEAMS, POOL, ROWS, LANES = 40, 12, 256, 128
 GROUP = 4
 LIMIT = 30 << 20
+FIRST, CHUNK = 16, 4
 EXACT = lax.Precision.HIGHEST
 NN = (((1,), (0,)), ((), ()))
 NT = (((1,), (1,)), ((), ()))
@@ -133,7 +135,9 @@
         ref[92:96, :] = jnp.zeros((4, ROWS), F32)
 
 
-def gram(w_ref, pool_ref, lap_ref, sums_ref, acc_ref):
+def gram(w_ref, pool_ref, lap_ref, sums_ref, lap_hbm, acc_ref, sem):
+    keep = pltpu.make_async_copy(lap_ref, lap_hbm, sem)
+    keep.start()
     acc_ref[...] = jnp.zeros_like(acc_ref)
 
     def pair(ref, count, t):
@@ -168,9 +172,26 @@
     to_l = jnp.where((i < BEAMS) & (lane == i + 40), 1.0, 0.0)
     sums = exact_dot(folded[0:16], to_p, NN) + exact_dot(folded[16:32], to_l, NN)
     sums_ref[...] = sums[0:POOL]
-
-
-def again(parts_ref, out_ref):
+    keep.wait()
+
+
+def cross(
+    sums_ref, row_a, row_b, row_a_got, row_b_got, col_a, col_b, col_a_got, col_b_got, sent_ref
+):
+    even_row = lax.axis_index(ROW[1]) == 0
+    even_col = (lax.axis_index(COL[1]) & 1) == 0
+    halo, edge = [], []
+    for even, got, own in ((even_col, (col_a_got, col_b_got), (col_a, col_b)), (even_row, (row_a_got, row_b_got), (row_a, row_b))):
+        halo.extend(by_side(even, *[ref[80:96, :] for ref in got]))
+        edge.extend(by_side(even, *[ref[0:40, :] for ref in own]))
+    edge = jnp.concatenate(edge, axis=1)
+    edge = jnp.concatenate([jnp.zeros((40, 768), F32), edge, jnp.zeros((48, 768), F32)], axis=0)
+    sums = sums_ref[...] + dot(jnp.concatenate(halo, axis=1), edge, NT, EXACT)[0:POOL]
+    for k in range(16):
+        sent_ref[k] = sums
+
+
+def again(parts_ref, token_ref, out_ref):
     sums = parts_ref[0]
     for k in range(1, 16):
         sums = sums + parts_ref[k]
@@ -178,12 +199,28 @@
         out_ref[k] = sums
 
 
-def base(
-    smooth_ref, active_ref, w_ref, pool_lap_ref, sums_ref, smooth_row_ref, active_row_ref,
-    row_a, row_b, row_a_got, row_b_got, col_a, col_b, col_a_got, col_b_got,
-    sent_ref, out_ref, lap_ref, fix_ref, turned_ref, slots_ref,
-    top_ref, bottom_ref, up_ref, down_ref, left_ref, right_ref, west_ref, east_ref,
-):
+def base(first, count, with_pool, smooth_ref, active_ref, w_hbm, lap_in_hbm, smooth_row_ref, active_row_ref, row_a, row_b, row_a_got, row_b_got, col_a, col_b, col_a_got, col_b_got, *rest):
+    if with_pool:
+        out_hbm, lap_hbm, token_ref, *rest, lap_ref = rest
+    else:
+        out_hbm, *rest = rest
+    (
+        fix_ref, turned_ref, slots_ref, top_ref, bottom_ref, up_ref, down_ref, left_ref, right_ref, west_ref, east_ref,
+        w_ref, out_ref, sems,
+    ) = rest
+    parts = count // CHUNK
+    loads, stores = [], []
+    for k in range(parts):
+        part = slice(CHUNK * k, CHUNK * (k + 1))
+        source = w_hbm.at[first + CHUNK * k : first + CHUNK * (k + 1)]
+        loads.append(pltpu.make_async_copy(source, w_ref.at[part], sems.at[0, k]))
+        stores.append(pltpu.make_async_copy(out_ref.at[part], out_hbm.at[part], sems.at[1, k]))
+    for copy in loads[:3]:
+        copy.start()
+    if with_pool:
+        load_lap = pltpu.make_async_copy(lap_in_hbm, lap_ref, sems.at[0, parts])
+        store_lap = pltpu.make_async_copy(lap_ref, lap_hbm, sems.at[1, parts])
+        load_lap.start()
     even_row = lax.axis_index(ROW[1]) == 0
     even_col = (lax.axis_index(COL[1]) & 1) == 0
     top_ref[...], bottom_ref[...] = by_side(even_row, row_a[...], row_b[...])
@@ -193,13 +230,6 @@
     for ref in (west_ref, east_ref):
         one, two = ref[96:136, 0:LANES], ref[96:136, LANES:]
         ref[96:136, 0:LANES], ref[96:136, LANES:] = by_side(even_row, one, two)
-    halo = jnp.concatenate([ref[80:96, :] for ref in (west_ref, east_ref, up_ref, down_ref)], axis=1)
-    edge = jnp.concatenate([ref[0:40, :] for ref in (left_ref, right_ref, top_ref, bottom_ref)], axis=1)
-    edge = jnp.concatenate([jnp.zeros((40, 768), F32), edge, jnp.zeros((48, 768), F32)], axis=0)
-    sums = sums_ref[...] + dot(halo, edge, NT, EXACT)[0:POOL]
-    for k in range(16):
-        sent_ref[k] = sums
-
     def across(row):
         return jnp.broadcast_to(row, (8, BEAMS)).T[:, 0:1]
 
@@ -265,14 +295,6 @@
         spun = pltpu.roll(slots_ref[image >> 5], (LANES - 2 - 4 * image) & (LANES - 1), 1)
         return jnp.where(at_edge, spun, 0.0)
 
-    def pool_step(p, carry):
-        lap_ref[p] = pool_lap_ref[p] + placed(BEAMS + p)
-        return carry
-
-    lax.fori_loop(0, POOL, pool_step, 0, unroll=4)
-    lap_ref[:, 0, :] += up_ref[80:92, :]
-    lap_ref[:, ROWS - 1, :] += down_ref[80:92, :]
-
     away = (iota((LANES, LANES), 0) - iota((LANES, LANES), 1)) & (LANES - 1)
     once = jnp.where(away == 0, -2.0, jnp.where((away == 1) | (away == LANES - 1), 1.0, 0.0))
     along = jnp.concatenate([once, dot(once, once, NN)], axis=1).astype(BF16)
@@ -282,7 +304,7 @@
         return pltpu.roll(x, 1, 0) + pltpu.roll(x, ROWS - 1, 0)
 
     def beam(b, carry):
-        s_b, n_b = smooth_ref[b], active_ref[b]
+        s_b, n_b = smooth_ref[first + b], active_ref[first + b]
         r_0, r_1 = jnp.where(n_b > 0, s_b, 0.0), jnp.where(n_b > 1, s_b, 0.0)
         a_b, c_b = r_0 + r_1, r_0 * r_1
         x = w_ref[b]
@@ -291,22 +313,61 @@
         lines = around(x)
         inner = around((a_b - 2.0 * c_b) * x + (2.0 * c_b) * one + c_b * lines)
         kept = (1.0 - 2.0 * a_b + 4.0 * c_b) * x + (a_b - 4.0 * c_b) * one + c_b * two - (2.0 * c_b) * lines
-        out = kept + inner + placed(b)
+        out = kept + inner + placed(first + b)
         out_ref[b, 8 : ROWS - 8, :] = out[8 : ROWS - 8]
-        out_ref[b, 0:8, :] = out[0:8] + fix_ref[b, :, 0:128]
-        out_ref[b, ROWS - 8 : ROWS, :] = out[ROWS - 8 :] + fix_ref[b, :, 128:256]
+        out_ref[b, 0:8, :] = out[0:8] + fix_ref[first + b, :, 0:128]
+        out_ref[b, ROWS - 8 : ROWS, :] = out[ROWS - 8 :] + fix_ref[first + b, :, 128:256]
         return carry
 
-    lax.fori_loop(0, BEAMS, beam, 0, unroll=2)
+    for k in range(parts):
+        loads[k].wait()
+        if k + 3 < parts:
+            loads[k + 3].start()
+        lax.fori_loop(CHUNK * k, CHUNK * (k + 1), beam, 0, unroll=2)
+        stores[k].start()
+        if k == 0 and with_pool:
+            load_lap.wait()
+
+            def pool_step(p, carry):
+                lap_ref[p] = lap_ref[p] + placed(BEAMS + p)
+                return carry
+
+            lax.fori_loop(0, POOL, pool_step, 0, unroll=4)
+            lap_ref[:, 0, :] += up_ref[80:92, :]
+            lap_ref[:, ROWS - 1, :] += down_ref[80:92, :]
+            store_lap.start()
+    for store in stores:
+        store.wait()
+    if with_pool:
+        store_lap.wait()
+        token_ref[...] = jnp.zeros_like(token_ref)
 
 
 def finish(
-    parts_ref, desired_ref, plan_ref, ref_ref, rate_ref, smooth_ref, active_ref, base_ref, pool_ref, lap_ref,
-    out_hbm, err_ref, done_ref, high_ref, low_ref, sems,
+    parts_ref, desired_ref, plan_ref, ref_ref, rate_ref, smooth_ref, active_ref, base_a_hbm, base_b_hbm, pool_hbm,
+    lap_hbm, out_hbm, err_ref, base_ref, pool_ref, lap_ref, high_ref, low_ref, in_sems, out_sems,
 ):
+    def rows_of(t):
+        return pl.ds(pl.multiple_of(t * 32, 8), 32)
+
+    def fetches(t):
+        cut = base_a_hbm.shape[0]
+        at = rows_of(t)
+        pairs = (
+            (base_a_hbm.at[:, at, :], base_ref.at[0:cut, at, :]),
+            (base_b_hbm.at[:, at, :], base_ref.at[cut:BEAMS, at, :]),
+            (pool_hbm.at[:, at, :], pool_ref.at[:, at, :]),
+            (lap_hbm.at[:, at, :], lap_ref.at[:, at, :]),
+        )
+        return [pltpu.make_async_copy(src, dst, in_sems.at[k, t]) for k, (src, dst) in enumerate(pairs)]
+
     def store(t):
-        at = pl.ds(pl.multiple_of(t * 32, 8), 32)
-        return pltpu.make_async_copy(done_ref.at[:, at, :], out_hbm.at[:, at, :], sems.at[t])
+        at = rows_of(t)
+        return pltpu.make_async_copy(base_ref.at[:, at, :], out_hbm.at[:, at, :], out_sems.at[t])
+
+    for t in range(8):
+        for copy in fetches(t):
+            copy.start()
 
     sums = parts_ref[0]
     for k in range(1, 16):
@@ -342,6 +403,9 @@
         ref[...] = jnp.where(same, dot(by_q, fold, NN), 0.0).astype(BF16)
 
     def step(t, carry):
+        for copy in fetches(t):
+            copy.wait()
+
         def tile(ref, at):
             return ref.at[:, pl.ds(pl.multiple_of(t * 32 + at, 8), 8), :]
 
@@ -356,8 +420,7 @@
             got = dot(high_ref[...], high, NN) + dot(high_ref[...], low, NN) + dot(low_ref[...], high, NN)
             for h in range(2):
                 part = got[:, h * LANES : (h + 1) * LANES].reshape(BEAMS, 8, LANES)
-                at = 16 * k + 8 * h
-                tile(done_ref, at)[...] = tile(base_ref, at)[...] + part
+                tile(base_ref, 16 * k + 8 * h)[...] += part
         store(t).start()
         return carry
 
@@ -369,7 +432,7 @@
 def call(kernel, outs, specs, scratch=(), out_specs=None):
     run = pl.pallas_call(
         kernel,
-        name=kernel.__name__,
+        name=getattr(kernel, "__name__", "base"),
         out_shape=outs,
         in_specs=specs,
         out_specs=out_specs or [VMEM] * len(outs),
@@ -421,33 +484,55 @@
     corners = jnp.concatenate([row_a_got[0:40], row_b_got[0:40]], axis=1)
     col_a_got = swapped(jnp.concatenate([col_a, corners], axis=0), COL, 0)
     col_b_got = swapped(jnp.concatenate([col_b, corners], axis=0), COL, 1)
-    (sums,) = call(gram, [vmem(POOL, LANES)], [VMEM] * 3, [vmem(416, 192)])(w_near, p_near, pool_lap)
+    sums, pool_lap = call(
+        gram,
+        [vmem(POOL, LANES), far_out(POOL, ROWS, LANES)],
+        [VMEM] * 3,
+        [vmem(416, 192), DMA],
+        [VMEM, HBM],
+    )(w_near, p_near, pool_lap)
+    edges = (row_a, row_b, row_a_got, row_b_got, col_a, col_b, col_a_got, col_b_got)
+    (sent,) = call(cross, [vmem(16, POOL, LANES)], [VMEM] * 9)(sums, *edges)
+    near = exchange(sent, NEAR)
     rows = (smoothing[None, :], active[None, :])
-    sent, based, lap = call(
-        base,
-        [vmem(16, POOL, LANES), vmem(BEAMS, ROWS, LANES), vmem(POOL, ROWS, LANES)],
-        [SMEM, SMEM] + [VMEM] * 13,
+    shared = (smoothing, active, weights, pool_lap, *rows, *edges)
+    specs = [SMEM, SMEM, HBM, HBM] + [VMEM] * 10
+    edge_scratch = (
         [vmem(BEAMS, 8, 256), vmem(2, 256, LANES), vmem(2, ROWS, LANES)]
-        + [vmem(96, LANES)] * 4 + [vmem(96, ROWS)] * 2 + [vmem(136, ROWS)] * 2,
-    )(
-        smoothing, active, w_near, pool_lap, sums, *rows,
-        row_a, row_b, row_a_got, row_b_got, col_a, col_b, col_a_got, col_b_got,
+        + [vmem(96, LANES)] * 4 + [vmem(96, ROWS)] * 2 + [vmem(136, ROWS)] * 2
     )
-    near = exchange(sent, NEAR)
-    (sent,) = call(again, [vmem(16, POOL, LANES)], [VMEM])(near)
+    rest = BEAMS - FIRST
+    based_a, lap, token = call(
+        functools.partial(base, 0, FIRST, True),
+        [far_out(FIRST, ROWS, LANES), far_out(POOL, ROWS, LANES), vmem(8, LANES)],
+        specs,
+        edge_scratch + [vmem(FIRST, ROWS, LANES)] * 2 + [DMA((2, FIRST // CHUNK + 1)), vmem(POOL, ROWS, LANES)],
+        [HBM, HBM, VMEM],
+    )(*shared)
+    (sent,) = call(again, [vmem(16, POOL, LANES)], [VMEM] * 2)(near, token)
     far = exchange(sent, FAR)
+    (based_b,) = call(
+        functools.partial(base, FIRST, rest, False),
+        [far_out(rest, ROWS, LANES)],
+        specs,
+        edge_scratch + [vmem(rest, ROWS, LANES)] * 2 + [DMA((2, rest // CHUNK))],
+        [HBM],
+    )(*shared)
     final, errors = call(
         finish,
         [far_out(BEAMS, ROWS, LANES), jax.ShapeDtypeStruct((2, 16, BEAMS), F32)],
-        [VMEM] * 10,
+        [VMEM] * 7 + [HBM] * 4,
         [
             vmem(BEAMS, ROWS, LANES),
+            vmem(POOL, ROWS, LANES),
+            vmem(POOL, ROWS, LANES),
             pltpu.VMEM((320, 192), BF16),
             pltpu.VMEM((320, 192), BF16),
+            DMA((4, 8)),
             DMA((8,)),
         ],
         [HBM, VMEM],
-    )(far, desired.T, plan, beam_ref[None, :], step_size[None, :], *rows, based, p_near, lap)
+    )(far, desired.T, plan, beam_ref[None, :], step_size[None, :], *rows, based_a, based_b, pool, lap)
     return final, jnp.swapaxes(errors, 1, 2)
 
 

time: 65.6 us -> 60 us (0.915)
  blocking collectives: 33.8 us -> 0 us
  starting transfers between devices: 4.67 us -> 22.6 us
  Pallas kernels: 25.9 us -> 32.8 us
  waiting for transfers between devices: 0.18 us -> 3.28 us
    all_to_all x2 -> x0, blocking collectives: 33.8 us -> none  [exchange(): return lax.all_to_all(value, axes, split_axis=0, concat_axis=0, tiled=True)]
    all_to_all x0 -> x2, starting transfers between devices: none -> 18 us  [exchange(): return lax.all_to_all(value, axes, split_axis=0, concat_axis=0, tiled=True)]
    pallas_call x6 -> x8, Pallas kernels: 25.9 us -> 32.8 us  [call(): run(*[at_home(x, spec) for x, spec in zip(args, specs)])]
    all_to_all x0 -> x2, waiting for transfers between devices: none -> 3.14 us  [exchange(): return lax.all_to_all(value, axes, split_axis=0, concat_axis=0, tiled=True)]
  transfers between devices with their start and end apart: 4 -> 6, of which waited for: 1 -> 3; matrix products, arithmetic and copies ran while one was open for 0% -> 0% of each run, Pallas kernels for 15% -> 39%
where the time goes in v3:
time: 60 us; the launch traced here: 59.6 us
  Pallas kernels  32.8 us (55%)
  starting transfers between devices  22.6 us (38%)
  waiting for transfers between devices  3.28 us (5%)
  between operations  0.83 us (1%)
    pallas_call x8, Pallas kernels, call(): run(*[at_home(x, spec) for x, spec in zip(args, specs)])  32.8 us
    all_to_all x2, starting transfers between devices, exchange(): return lax.all_to_all(value, axes, split_axis=0, concat_axis=0, tiled=True)  18 us
    ppermute x4, starting transfers between devices, swapped(): return lax.ppermute(value, axes, pairs + [(b, a) for a, b in pairs])  4.67 us
    all_to_all x2, waiting for transfers between devices, exchange(): return lax.all_to_all(value, axes, split_axis=0, concat_axis=0, tiled=True)  3.14 us
  transfers between devices with their start and end apart: 6, of which 3 were waited for; matrix products, arithmetic and copies ran while one was open for 0% of the time, Pallas kernels for 39%

profile of v3, /device:TPU:32, one launch (start us, length us, event | category | flops | bytes accessed | tf_op | source)
XLA Modules:
  0.0 59.6 jit_solution(6162142316086208851)
XLA Ops:
  0.6 1.1 %line_ends.1 = (f32[96,128]{1,0:T(8,128)S(1)}, f32[96,128]{1,0:T(8,128)S(1)}) custom-call(f32[40,256,128]{2,1,0:T(8,128)} %w_hbm.7, f32[12,256,128]{2,1,0:T(8,128)} %pool_hbm.5), custom_call_target="tpu_custom_call" | custom-call | tf_op jit(solution)/shard_map/line_ends/pallas_call | solution.py:447
  1.8 0.1 collective-permute-start
  1.9 0.7 %collective-permute-start.1 = (f32[96,128]{1,0:T(8,128)S(1)}, f32[96,128]{1,0:T(8,128)S(1)}, u32[]{:S(2)}, u32[]{:S(2)}) collective-permute-start(f32[96,128]{1,0:T(8,128)S(1)} %get-tuple-element.21.row_b), channel_id=1, source_target_pairs={{32,64},{96,128},{160,192},{64,32},{128,96},{192,160},{33,65},{97,... | collective-permute-start | bytes 147464 | tf_op jit(solution)/shard_map/ppermute | solution.py:461
  2.6 5.2 %column_ends.1 = (f32[96,256]{1,0:T(8,128)S(1)}, f32[96,256]{1,0:T(8,128)S(1)}, f32[40,256,128]{2,1,0:T(8,128)S(1)}, f32[12,256,128]{2,1,0:T(8,128)S(1)}, f32[12,256,128]{2,1,0:T(8,128)S(1)}) custom-call(f32[40,256,128]{2,1,0:T(8,128)} %w_hbm.7, f32[12,256,128]{2,1,0:T(8,128)} %pool_hbm.5), custom_call_target="tpu_custom_call" | custom-call | tf_op jit(solution)/shard_map/column_ends/pallas_call | solution.py:447
  7.7 0.0 collective-permute-done.row_a_got
  7.8 0.0 collective-permute-done.1.row_b_got
  7.8 3.8 %collective-permute-start.3 = (f32[136,256]{1,0:T(8,128)S(1)}, f32[136,256]{1,0:T(8,128)S(1)}, u32[]{:S(2)}, u32[]{:S(2)}) collective-permute-start(f32[136,256]{1,0:T(8,128)S(1)} %get-tuple-element.30), channel_id=1, source_target_pairs={{1,2},{3,4},{5,6},{7,8},{9,10},{11,12},{13,14},{15,16},{17,18},{19... | collective-permute-start | bytes 417800 | tf_op jit(solution)/shard_map/ppermute | solution.py:461
  11.6 0.1 collective-permute-start.2
  11.7 0.0 copy-start
  11.8 0.0 copy-start.1
  11.8 4.9 %gram.1 = (f32[12,128]{1,0:T(8,128)S(1)}, f32[12,256,128]{2,1,0:T(8,128)}) custom-call(f32[40,256,128]{2,1,0:T(8,128)S(1)} %get-tuple-element.16.w_ref, f32[12,256,128]{2,1,0:T(8,128)S(1)} %get-tuple-element.17.pool_ref, f32[12,256,128]{2,1,0:T(8,128)S(1)} %get-tuple-element.18.lap_ref), custom_call_target="tpu_custom_call" | custom-call | tf_op jit(solution)/shard_map/gram/pallas_call | solution.py:447
  16.6 0.0 collective-permute-done.3.col_b_got
  16.7 0.1 collective-permute-done.2.col_a_got
  16.8 1.0 %cross.1 = f32[16,12,128]{2,1,0:T(8,128)} custom-call(f32[12,128]{1,0:T(8,128)S(1)} %get-tuple-element.19.sums_ref, f32[96,128]{1,0:T(8,128)S(1)} %get-tuple-element.20.row_a, f32[96,128]{1,0:T(8,128)S(1)} %get-tuple-element.21.row_b, f32[96,128]{1,0:T(8,128)S(1)} %collective-permute-done.row_a_got, f32[96,128]{1,0:T(8,128)S(1)} %collective-permute-done.1.row_b_got, ...), custom_call_target="tpu_custom_call" | custom-call | tf_op jit(solution)/shard_map/cross/pallas_call | solution.py:447
  17.8 10.5 %all-to-all-start = ((f32[16,12,128]{2,1,0:T(8,128)}), f32[16,12,128]{2,1,0:T(8,128)S(1)}, u32[]{:S(2)}, u32[]{:S(2)}) async-start(f32[16,12,128]{2,1,0:T(8,128)} %cross.1), calls=%async_computation | async-start | bytes 262144 | tf_op jit(solution)/shard_map/all_to_all | solution.py:465
  28.3 0.0 copy-done
  28.3 0.0 copy-done.1
  28.3 6.3 %base.2 = (f32[16,256,128]{2,1,0:T(8,128)}, f32[12,256,128]{2,1,0:T(8,128)}, f32[8,128]{1,0:T(8,128)S(1)}) custom-call(f32[40]{0:T(128)S(1)} %copy-done, s32[40]{0:T(128)S(1)} %copy-done.1, f32[40,256,128]{2,1,0:T(8,128)} %w_hbm.7, f32[12,256,128]{2,1,0:T(8,128)} %get-tuple-element.24.lap_in_hbm, f32[1,40]{1,0:T(1,128)S(1)} %bitcast.6, s32[1,40]{1,0:T(1,128)S(1)} %bitcast.9, ...), custom_call_target="tpu_custom_call" | custom-call | tf_op jit(solution)/shard_map/base/pallas_call | solution.py:447
  34.6 1.9 %all-to-all-done.parts_ref = f32[16,12,128]{2,1,0:T(8,128)S(1)} async-done(((f32[16,12,128]{2,1,0:T(8,128)}), f32[16,12,128]{2,1,0:T(8,128)S(1)}, u32[]{:S(2)}, u32[]{:S(2)}) %all-to-all-start) | async-done | bytes 98336 | tf_op jit(solution)/shard_map/all_to_all | solution.py:465
  36.5 0.7 %again.1 = f32[16,12,128]{2,1,0:T(8,128)} custom-call(f32[16,12,128]{2,1,0:T(8,128)S(1)} %all-to-all-done.parts_ref, f32[8,128]{1,0:T(8,128)S(1)} %get-tuple-element.25.token_ref), custom_call_target="tpu_custom_call" | custom-call | tf_op jit(solution)/shard_map/again/pallas_call | solution.py:447
  37.1 7.4 %all-to-all-start.1 = ((f32[16,12,128]{2,1,0:T(8,128)}), f32[16,12,128]{2,1,0:T(8,128)S(1)}, u32[]{:S(2)}, u32[]{:S(2)}) async-start(f32[16,12,128]{2,1,0:T(8,128)} %again.1), calls=%async_computation.1 | async-start | bytes 262144 | tf_op jit(solution)/shard_map/all_to_all | solution.py:465
  44.6 0.0 copy-start.2
  44.6 0.0 copy-start.3
  44.6 0.0 copy-start.4
  44.6 0.0 copy-start.5
  44.6 6.7 %base.3.base_b_hbm = f32[24,256,128]{2,1,0:T(8,128)} custom-call(f32[40]{0:T(128)S(1)} %copy-done, s32[40]{0:T(128)S(1)} %copy-done.1, f32[40,256,128]{2,1,0:T(8,128)} %w_hbm.7, f32[12,256,128]{2,1,0:T(8,128)} %get-tuple-element.24.lap_in_hbm, f32[1,40]{1,0:T(1,128)S(1)} %bitcast.7, s32[1,40]{1,0:T(1,128)S(1)} %bitcast.10, ...), custom_call_target="tpu_custom_call" | custom-call | tf_op jit(solution)/shard_map/base/pallas_call | solution.py:447
  51.4 1.2 %all-to-all-done.1.parts_ref = f32[16,12,128]{2,1,0:T(8,128)S(1)} async-done(((f32[16,12,128]{2,1,0:T(8,128)}), f32[16,12,128]{2,1,0:T(8,128)S(1)}, u32[]{:S(2)}, u32[]{:S(2)}) %all-to-all-start.1) | async-done | bytes 98336 | tf_op jit(solution)/shard_map/all_to_all | solution.py:465
  52.6 0.0 copy-done.2
  52.6 0.0 copy-done.3
  52.6 0.0 copy-done.4
  52.6 0.0 copy-done.5
  52.6 7.0 %finish.1 = (f32[40,256,128]{2,1,0:T(8,128)}, f32[2,16,40]{2,1,0:T(8,128)}) custom-call(f32[16,12,128]{2,1,0:T(8,128)S(1)} %all-to-all-done.1.parts_ref, f32[8,12]{1,0:T(8,128)S(1)} %bitcast.12, s32[2,16]{1,0:T(2,128)S(1)} %copy-done.3, s32[1,40]{1,0:T(1,128)S(1)} %bitcast.13, f32[1,40]{1,0:T(1,128)S(1)} %bitcast.14, f32[1,40]{1,0:T(1,128)S(1)} %bitcast.8, ...), custom_call_target="tpu_custom_call" | custom-call | tf_op jit(solution)/shard_map/finish/pallas_call | solution.py:447
  (3 shorter events, 0.0 us)
Async XLA Ops:
  1.8 6.0 %collective-permute-start = (f32[96,128]{1,0:T(8,128)S(1)}, f32[96,128]{1,0:T(8,128)S(1)}, u32[]{:S(2)}, u32[]{:S(2)}) collective-permute-start(f32[96,128]{1,0:T(8,128)S(1)} %get-tuple-element.20.row_a), channel_id=1, source_target_pairs={{0,32},{64,96},{128,160},{192,224},{32,0},{96,64},{160,128},{224,1... | collective-permute-start | bytes 147464 | tf_op jit(solution)/shard_map/ppermute | solution.py:461
  1.9 5.9 %collective-permute-start.1 = (f32[96,128]{1,0:T(8,128)S(1)}, f32[96,128]{1,0:T(8,128)S(1)}, u32[]{:S(2)}, u32[]{:S(2)}) collective-permute-start(f32[96,128]{1,0:T(8,128)S(1)} %get-tuple-element.21.row_b), channel_id=1, source_target_pairs={{32,64},{96,128},{160,192},{64,32},{128,96},{192,160},{33,65},{97,... | collective-permute-start | bytes 147464 | tf_op jit(solution)/shard_map/ppermute | solution.py:461
  7.8 8.8 %collective-permute-start.3 = (f32[136,256]{1,0:T(8,128)S(1)}, f32[136,256]{1,0:T(8,128)S(1)}, u32[]{:S(2)}, u32[]{:S(2)}) collective-permute-start(f32[136,256]{1,0:T(8,128)S(1)} %get-tuple-element.30), channel_id=1, source_target_pairs={{1,2},{3,4},{5,6},{7,8},{9,10},{11,12},{13,14},{15,16},{17,18},{19... | collective-permute-start | bytes 417800 | tf_op jit(solution)/shard_map/ppermute | solution.py:461
  11.6 5.1 %collective-permute-start.2 = (f32[136,256]{1,0:T(8,128)S(1)}, f32[136,256]{1,0:T(8,128)S(1)}, u32[]{:S(2)}, u32[]{:S(2)}) collective-permute-start(f32[136,256]{1,0:T(8,128)S(1)} %get-tuple-element.31), channel_id=1, source_target_pairs={{0,1},{2,3},{4,5},{6,7},{8,9},{10,11},{12,13},{14,15},{16,17},{18,... | collective-permute-start | bytes 417800 | tf_op jit(solution)/shard_map/ppermute | solution.py:461
  11.7 16.5 %copy-start = (f32[40]{0:T(128)S(1)}, f32[40]{0:T(128)}, u32[]{:S(2)}) copy-start(f32[40]{0:T(128)} %smooth_ref.3) | copy-start | bytes 484
  11.8 16.5 %copy-start.1 = (s32[40]{0:T(128)S(1)}, s32[40]{0:T(128)}, u32[]{:S(2)}) copy-start(s32[40]{0:T(128)} %active_ref.3) | copy-start | bytes 484
  17.8 18.7 %all-to-all-start = ((f32[16,12,128]{2,1,0:T(8,128)}), f32[16,12,128]{2,1,0:T(8,128)S(1)}, u32[]{:S(2)}, u32[]{:S(2)}) async-start(f32[16,12,128]{2,1,0:T(8,128)} %cross.1), calls=%async_computation | async-start | bytes 262144 | tf_op jit(solution)/shard_map/all_to_all | solution.py:465
  37.1 15.4 %all-to-all-start.1 = ((f32[16,12,128]{2,1,0:T(8,128)}), f32[16,12,128]{2,1,0:T(8,128)S(1)}, u32[]{:S(2)}, u32[]{:S(2)}) async-start(f32[16,12,128]{2,1,0:T(8,128)} %again.1), calls=%async_computation.1 | async-start | bytes 262144 | tf_op jit(solution)/shard_map/all_to_all | solution.py:465
  44.6 8.0 %copy-start.2 = (f32[12,8]{0,1:T(8,128)S(1)}, f32[12,8]{0,1:T(8,128)}, u32[]{:S(2)}) copy-start(f32[12,8]{0,1:T(8,128)} %param.10) | copy-start | bytes 1156
  44.6 8.0 %copy-start.3 = (s32[2,16]{1,0:T(2,128)S(1)}, s32[2,16]{1,0:T(2,128)}, u32[]{:S(2)}) copy-start(s32[2,16]{1,0:T(2,128)} %plan_ref.1) | copy-start | bytes 388
  44.6 8.0 %copy-start.4 = (s32[40]{0:T(128)S(1)}, s32[40]{0:T(128)}, u32[]{:S(2)}) copy-start(s32[40]{0:T(128)} %param.12) | copy-start | bytes 484
  44.6 8.0 %copy-start.5 = (f32[40]{0:T(128)S(1)}, f32[40]{0:T(128)}, u32[]{:S(2)}) copy-start(f32[40]{0:T(128)} %param.13) | copy-start | bytes 484

commit v4 on v3

--- a/solution.py
+++ b/solution.py
@@ -17,7 +17,7 @@
 FAR = ("row_0", "col_0")
 SCALE = 1.0 / math.sqrt(NR * NC)
 BEAMS, POOL, ROWS, LANES = 40, 12, 256, 128
-GROUP = 4
+GROUP = 8
 LIMIT = 30 << 20
 FIRST, CHUNK = 16, 4
 EXACT = lax.Precision.HIGHEST
@@ -90,7 +90,7 @@
         ref[92:96, :] = jnp.zeros((4, LANES), F32)
 
 
-def column_ends(w_hbm, pool_hbm, first_ref, second_ref, w_buf, pool_buf, lap_ref, ends_ref, sems):
+def column_ends(w_hbm, pool_hbm, first_ref, second_ref, w_buf, pool_buf, ends_ref, sems):
     copies = [pltpu.make_async_copy(pool_hbm, pool_buf, sems.at[5])]
     for k in range(5):
         copies.append(pltpu.make_async_copy(w_hbm.at[8 * k : 8 * k + 8], w_buf.at[8 * k : 8 * k + 8], sems.at[k]))
@@ -102,14 +102,9 @@
         pick = jnp.where((row == k) & (lane == spot), 1.0, pick)
     pick = pick.astype(BF16)
     pick = jnp.concatenate([pick, pick], axis=1)
-    along = band_matrix(-4.0).astype(BF16)
-    along = jnp.concatenate([along, along], axis=0)
-
     def image(p, carry):
         x = pool_buf[p]
-        both = jnp.concatenate(halves(x), axis=1)
-        ends_ref[BEAMS + p] = dot(pick, both, NT)
-        lap_ref[p] = rows_around(x) + dot(both, along, NN)
+        ends_ref[BEAMS + p] = dot(pick, jnp.concatenate(halves(x), axis=1), NT)
         return carry
 
     def beam(b, carry):
@@ -135,7 +130,16 @@
         ref[92:96, :] = jnp.zeros((4, ROWS), F32)
 
 
-def gram(w_ref, pool_ref, lap_ref, sums_ref, lap_hbm, acc_ref, sem):
+def gram(w_ref, pool_ref, sums_ref, lap_hbm, acc_ref, lap_ref, sem):
+    along = band_matrix(-4.0).astype(BF16)
+    along = jnp.concatenate([along, along], axis=0)
+
+    def image(p, carry):
+        x = pool_ref[p]
+        lap_ref[p] = rows_around(x) + dot(jnp.concatenate(halves(x), axis=1), along, NN)
+        return carry
+
+    lax.fori_loop(0, POOL, image, 0, unroll=4)
     keep = pltpu.make_async_copy(lap_ref, lap_hbm, sem)
     keep.start()
     acc_ref[...] = jnp.zeros_like(acc_ref)
@@ -187,8 +191,9 @@
     edge = jnp.concatenate(edge, axis=1)
     edge = jnp.concatenate([jnp.zeros((40, 768), F32), edge, jnp.zeros((48, 768), F32)], axis=0)
     sums = sums_ref[...] + dot(jnp.concatenate(halo, axis=1), edge, NT, EXACT)[0:POOL]
+    flat = jnp.concatenate([sums[p : p + 1] for p in range(POOL)], axis=1)
     for k in range(16):
-        sent_ref[k] = sums
+        sent_ref[k] = flat
 
 
 def again(parts_ref, token_ref, out_ref):
@@ -199,15 +204,14 @@
         out_ref[k] = sums
 
 
-def base(first, count, with_pool, smooth_ref, active_ref, w_hbm, lap_in_hbm, smooth_row_ref, active_row_ref, row_a, row_b, row_a_got, row_b_got, col_a, col_b, col_a_got, col_b_got, *rest):
+def base(first, count, with_pool, smooth_ref, active_ref, w_hbm, lap_in_hbm, *rest):
     if with_pool:
-        out_hbm, lap_hbm, token_ref, *rest, lap_ref = rest
+        smooth_row_ref, active_row_ref, row_a, row_b, row_a_got, row_b_got, *rest = rest
+        col_a, col_b, col_a_got, col_b_got, *rest = rest
+        out_hbm, lap_hbm, fix_ref, slots_ref, turned_ref, *rest, lap_ref = rest
+        top_ref, bottom_ref, up_ref, down_ref, left_ref, right_ref, west_ref, east_ref, w_ref, out_ref, sems = rest
     else:
-        out_hbm, *rest = rest
-    (
-        fix_ref, turned_ref, slots_ref, top_ref, bottom_ref, up_ref, down_ref, left_ref, right_ref, west_ref, east_ref,
-        w_ref, out_ref, sems,
-    ) = rest
+        fix_ref, slots_ref, out_hbm, w_ref, out_ref, sems = rest
     parts = count // CHUNK
     loads, stores = [], []
     for k in range(parts):
@@ -221,73 +225,74 @@
         load_lap = pltpu.make_async_copy(lap_in_hbm, lap_ref, sems.at[0, parts])
         store_lap = pltpu.make_async_copy(lap_ref, lap_hbm, sems.at[1, parts])
         load_lap.start()
-    even_row = lax.axis_index(ROW[1]) == 0
-    even_col = (lax.axis_index(COL[1]) & 1) == 0
-    top_ref[...], bottom_ref[...] = by_side(even_row, row_a[...], row_b[...])
-    up_ref[...], down_ref[...] = by_side(even_row, row_a_got[...], row_b_got[...])
-    left_ref[...], right_ref[...] = by_side(even_col, col_a[...], col_b[...])
-    west_ref[...], east_ref[...] = by_side(even_col, col_a_got[...], col_b_got[...])
-    for ref in (west_ref, east_ref):
-        one, two = ref[96:136, 0:LANES], ref[96:136, LANES:]
-        ref[96:136, 0:LANES], ref[96:136, LANES:] = by_side(even_row, one, two)
-    def across(row):
-        return jnp.broadcast_to(row, (8, BEAMS)).T[:, 0:1]
-
-    smooth_row, active_row = smooth_row_ref[...], active_row_ref[...]
-    live0 = jnp.where(active_row > 0, 1.0, 0.0)
-    live1 = jnp.where(active_row > 1, 1.0, 0.0)
-    a = across(smooth_row * (live0 + live1))
-    c = across(smooth_row * smooth_row * live0 * live1)
-    r = lax.axis_index(ROW[0]) * 2 + lax.axis_index(ROW[1])
-    k = lax.axis_index(COL[0]) * 8 + lax.axis_index(COL[1])
-    has_up, has_down = jnp.where(r > 0, 1.0, 0.0), jnp.where(r < 7, 1.0, 0.0)
-    has_west, has_east = jnp.where(k > 0, 1.0, 0.0), jnp.where(k < 31, 1.0, 0.0)
-    span, shifted, corner = slice(0, 40), slice(40, 80), slice(96, 136)
-    wide, thin = iota((BEAMS, ROWS), 1), iota((BEAMS, LANES), 1)
-
-    def mixed(near, far, own, prev, after):
-        return a * near + c * (2.0 * (prev + after) - 8.0 * near + far + own), c * near
-
-    def column(msg_ref, own_ref, far_ref, has):
-        near = msg_ref[span, :] - far_ref[span, :]
-        prev = jnp.where(wide == 0, 0.0, pltpu.roll(near, 1, 1))
-        after = jnp.where(wide == ROWS - 1, 0.0, pltpu.roll(near, ROWS - 1, 1))
-        far = msg_ref[shifted, :] - far_ref[shifted, :]
-        return mixed(near, far, (has - 1.0) * own_ref[span, :], prev, after)
-
-    def line(msg_ref, own_ref, far_ref, has, at):
-        near = msg_ref[span, :] - far_ref[span, :]
-        west = pltpu.roll(west_ref[corner, at : at + LANES] - far_ref[span, :], 1, 1)
-        east = pltpu.roll(east_ref[corner, at : at + LANES] - far_ref[span, :], LANES - 1, 1)
-        prev = jnp.where(thin == 0, west, pltpu.roll(near, 1, 1))
-        after = jnp.where(thin == LANES - 1, east, pltpu.roll(near, LANES - 1, 1))
-        far = msg_ref[shifted, :] - far_ref[shifted, :]
-        return mixed(near, far, (has - 1.0) * own_ref[span, :], prev, after)
-
-    fix_ref[...] = jnp.zeros_like(fix_ref)
-    turned_ref[...] = jnp.zeros_like(turned_ref)
-
-    def beams_at(k):
-        return pl.ds(k, BEAMS, stride=4)
-
-    def pools_at(k):
-        return pl.ds(4 * BEAMS + k, POOL, stride=4)
-
-    east, west = column(east_ref, right_ref, left_ref, has_east), column(west_ref, left_ref, right_ref, has_west)
-    for k, (line_of, pool_of) in enumerate(
-        ((east[1], None), (east[0], east_ref[80:92, :]), (west[0], west_ref[80:92, :]), (west[1], None))
-    ):
-        for h in range(2):
-            part = slice(LANES * h, LANES * (h + 1))
-            turned_ref[h, beams_at(k), :] = line_of[:, part]
-            if pool_of is not None:
-                turned_ref[h, pools_at(k), :] = pool_of[:, part]
-    for k in range(2):
-        for h in range(2):
-            part = slice(LANES * h, LANES * (h + 1))
-            slots_ref[k, part, :] = turned_ref[h, LANES * k : LANES * (k + 1), :].T
-    fix_ref[:, 0, 0:128], fix_ref[:, 1, 0:128] = line(up_ref, top_ref, bottom_ref, has_up, 0)
-    fix_ref[:, 7, 128:256], fix_ref[:, 6, 128:256] = line(down_ref, bottom_ref, top_ref, has_down, LANES)
+    if with_pool:
+        even_row = lax.axis_index(ROW[1]) == 0
+        even_col = (lax.axis_index(COL[1]) & 1) == 0
+        top_ref[...], bottom_ref[...] = by_side(even_row, row_a[...], row_b[...])
+        up_ref[...], down_ref[...] = by_side(even_row, row_a_got[...], row_b_got[...])
+        left_ref[...], right_ref[...] = by_side(even_col, col_a[...], col_b[...])
+        west_ref[...], east_ref[...] = by_side(even_col, col_a_got[...], col_b_got[...])
+        for ref in (west_ref, east_ref):
+            one, two = ref[96:136, 0:LANES], ref[96:136, LANES:]
+            ref[96:136, 0:LANES], ref[96:136, LANES:] = by_side(even_row, one, two)
+        def across(row):
+            return jnp.broadcast_to(row, (8, BEAMS)).T[:, 0:1]
+
+        smooth_row, active_row = smooth_row_ref[...], active_row_ref[...]
+        live0 = jnp.where(active_row > 0, 1.0, 0.0)
+        live1 = jnp.where(active_row > 1, 1.0, 0.0)
+        a = across(smooth_row * (live0 + live1))
+        c = across(smooth_row * smooth_row * live0 * live1)
+        r = lax.axis_index(ROW[0]) * 2 + lax.axis_index(ROW[1])
+        k = lax.axis_index(COL[0]) * 8 + lax.axis_index(COL[1])
+        has_up, has_down = jnp.where(r > 0, 1.0, 0.0), jnp.where(r < 7, 1.0, 0.0)
+        has_west, has_east = jnp.where(k > 0, 1.0, 0.0), jnp.where(k < 31, 1.0, 0.0)
+        span, shifted, corner = slice(0, 40), slice(40, 80), slice(96, 136)
+        wide, thin = iota((BEAMS, ROWS), 1), iota((BEAMS, LANES), 1)
+
+        def mixed(near, far, own, prev, after):
+            return a * near + c * (2.0 * (prev + after) - 8.0 * near + far + own), c * near
+
+        def column(msg_ref, own_ref, far_ref, has):
+            near = msg_ref[span, :] - far_ref[span, :]
+            prev = jnp.where(wide == 0, 0.0, pltpu.roll(near, 1, 1))
+            after = jnp.where(wide == ROWS - 1, 0.0, pltpu.roll(near, ROWS - 1, 1))
+            far = msg_ref[shifted, :] - far_ref[shifted, :]
+            return mixed(near, far, (has - 1.0) * own_ref[span, :], prev, after)
+
+        def line(msg_ref, own_ref, far_ref, has, at):
+            near = msg_ref[span, :] - far_ref[span, :]
+            west = pltpu.roll(west_ref[corner, at : at + LANES] - far_ref[span, :], 1, 1)
+            east = pltpu.roll(east_ref[corner, at : at + LANES] - far_ref[span, :], LANES - 1, 1)
+            prev = jnp.where(thin == 0, west, pltpu.roll(near, 1, 1))
+            after = jnp.where(thin == LANES - 1, east, pltpu.roll(near, LANES - 1, 1))
+            far = msg_ref[shifted, :] - far_ref[shifted, :]
+            return mixed(near, far, (has - 1.0) * own_ref[span, :], prev, after)
+
+        fix_ref[...] = jnp.zeros_like(fix_ref)
+        turned_ref[...] = jnp.zeros_like(turned_ref)
+
+        def beams_at(k):
+            return pl.ds(k, BEAMS, stride=4)
+
+        def pools_at(k):
+            return pl.ds(4 * BEAMS + k, POOL, stride=4)
+
+        east, west = column(east_ref, right_ref, left_ref, has_east), column(west_ref, left_ref, right_ref, has_west)
+        for k, (line_of, pool_of) in enumerate(
+            ((east[1], None), (east[0], east_ref[80:92, :]), (west[0], west_ref[80:92, :]), (west[1], None))
+        ):
+            for h in range(2):
+                part = slice(LANES * h, LANES * (h + 1))
+                turned_ref[h, beams_at(k), :] = line_of[:, part]
+                if pool_of is not None:
+                    turned_ref[h, pools_at(k), :] = pool_of[:, part]
+        for k in range(2):
+            for h in range(2):
+                part = slice(LANES * h, LANES * (h + 1))
+                slots_ref[k, part, :] = turned_ref[h, LANES * k : LANES * (k + 1), :].T
+        fix_ref[:, 0, 0:128], fix_ref[:, 1, 0:128] = line(up_ref, top_ref, bottom_ref, has_up, 0)
+        fix_ref[:, 7, 128:256], fix_ref[:, 6, 128:256] = line(down_ref, bottom_ref, top_ref, has_down, LANES)
     lane = iota((ROWS, LANES), 1)
     at_edge = (lane < 2) | (lane >= LANES - 2)
 
@@ -323,7 +328,7 @@
         loads[k].wait()
         if k + 3 < parts:
             loads[k + 3].start()
-        lax.fori_loop(CHUNK * k, CHUNK * (k + 1), beam, 0, unroll=2)
+        lax.fori_loop(CHUNK * k, CHUNK * (k + 1), beam, 0, unroll=4)
         stores[k].start()
         if k == 0 and with_pool:
             load_lap.wait()
@@ -340,7 +345,6 @@
         store.wait()
     if with_pool:
         store_lap.wait()
-        token_ref[...] = jnp.zeros_like(token_ref)
 
 
 def finish(
@@ -372,6 +376,7 @@
     sums = parts_ref[0]
     for k in range(1, 16):
         sums = sums + parts_ref[k]
+    sums = jnp.concatenate([sums[:, LANES * p : LANES * (p + 1)] for p in range(POOL)], axis=0)
     one_hot = jnp.where(iota((8, BEAMS), 0) == ref_ref[...], 1.0, 0.0)
     target = dot(desired_ref[...], one_hot, TN, EXACT)
     rate, smooth = rate_ref[...] * SCALE, smooth_ref[...]
@@ -387,8 +392,6 @@
     p1 = p0 + live0 * (rate * dot(inner, c0, NN, EXACT) + smooth * lap)
     e1 = target - SCALE * p1
     c1 = many[1] * e1
-    for t, e in enumerate((e0, e1)):
-        err_ref[t] = dot(hits[t], e, TN, EXACT)
     d0 = rate * (live0 * c0 + live1 * c1)
     d1 = live0 * live1 * rate * smooth * c0
     gap = jnp.zeros((4, BEAMS), F32)
@@ -425,6 +428,8 @@
         return carry
 
     lax.fori_loop(0, 8, step, 0)
+    for t, e in enumerate((e0, e1)):
+        err_ref[t] = dot(hits[t], e, TN, EXACT)
     for t in range(8):
         store(t).wait()
 
@@ -475,9 +480,9 @@
     )(weights, pool)
     row_b_got = swapped(row_b, ROW, 1)
     row_a_got = swapped(row_a, ROW, 0)
-    col_a, col_b, w_near, p_near, pool_lap = call(
+    col_a, col_b, w_near, p_near = call(
         column_ends,
-        [vmem(96, ROWS)] * 2 + [vmem(BEAMS, ROWS, LANES), vmem(POOL, ROWS, LANES), vmem(POOL, ROWS, LANES)],
+        [vmem(96, ROWS)] * 2 + [vmem(BEAMS, ROWS, LANES), vmem(POOL, ROWS, LANES)],
         [HBM, HBM],
         [vmem(BEAMS + POOL, 8, ROWS), DMA((6,))],
     )(weights, pool)
@@ -487,37 +492,41 @@
     sums, pool_lap = call(
         gram,
         [vmem(POOL, LANES), far_out(POOL, ROWS, LANES)],
-        [VMEM] * 3,
-        [vmem(416, 192), DMA],
+        [VMEM] * 2,
+        [vmem(416, 192), vmem(POOL, ROWS, LANES), DMA],
         [VMEM, HBM],
-    )(w_near, p_near, pool_lap)
+    )(w_near, p_near)
     edges = (row_a, row_b, row_a_got, row_b_got, col_a, col_b, col_a_got, col_b_got)
-    (sent,) = call(cross, [vmem(16, POOL, LANES)], [VMEM] * 9)(sums, *edges)
+    (sent,) = call(cross, [vmem(16, 1, POOL * LANES)], [VMEM] * 9)(sums, *edges)
     near = exchange(sent, NEAR)
     rows = (smoothing[None, :], active[None, :])
     shared = (smoothing, active, weights, pool_lap, *rows, *edges)
     specs = [SMEM, SMEM, HBM, HBM] + [VMEM] * 10
     edge_scratch = (
-        [vmem(BEAMS, 8, 256), vmem(2, 256, LANES), vmem(2, ROWS, LANES)]
-        + [vmem(96, LANES)] * 4 + [vmem(96, ROWS)] * 2 + [vmem(136, ROWS)] * 2
+        [vmem(2, 256, LANES)] + [vmem(96, LANES)] * 4 + [vmem(96, ROWS)] * 2 + [vmem(136, ROWS)] * 2
     )
     rest = BEAMS - FIRST
-    based_a, lap, token = call(
+    based_a, lap, fix, slots = call(
         functools.partial(base, 0, FIRST, True),
-        [far_out(FIRST, ROWS, LANES), far_out(POOL, ROWS, LANES), vmem(8, LANES)],
+        [
+            far_out(FIRST, ROWS, LANES),
+            far_out(POOL, ROWS, LANES),
+            vmem(BEAMS, 8, 256),
+            vmem(2, ROWS, LANES),
+        ],
         specs,
         edge_scratch + [vmem(FIRST, ROWS, LANES)] * 2 + [DMA((2, FIRST // CHUNK + 1)), vmem(POOL, ROWS, LANES)],
-        [HBM, HBM, VMEM],
+        [HBM, HBM, VMEM, VMEM],
     )(*shared)
-    (sent,) = call(again, [vmem(16, POOL, LANES)], [VMEM] * 2)(near, token)
+    (sent,) = call(again, [vmem(16, 1, POOL * LANES)], [VMEM] * 2)(near, slots)
     far = exchange(sent, FAR)
     (based_b,) = call(
         functools.partial(base, FIRST, rest, False),
         [far_out(rest, ROWS, LANES)],
-        specs,
-        edge_scratch + [vmem(rest, ROWS, LANES)] * 2 + [DMA((2, rest // CHUNK))],
+        [SMEM, SMEM, HBM, HBM, VMEM, VMEM],
+        [vmem(rest, ROWS, LANES)] * 2 + [DMA((2, rest // CHUNK))],
         [HBM],
-    )(*shared)
+    )(smoothing, active, weights, pool_lap, fix, slots)
     final, errors = call(
         finish,
         [far_out(BEAMS, ROWS, LANES), jax.ShapeDtypeStruct((2, 16, BEAMS), F32)],

time: 60 us -> 59 us (0.983)
  Pallas kernels: 32.8 us -> 31.8 us
    pallas_call x8, Pallas kernels: 32.8 us -> 31.8 us  [call(): run(*[at_home(x, spec) for x, spec in zip(args, specs)])]
  transfers between devices with their start and end apart: 6 -> 6, of which waited for: 3 -> 2; matrix products, arithmetic and copies ran while one was open for 0% -> 0% of each run, Pallas kernels for 39% -> 38%
where the time goes in v4:
time: 59 us; the launch traced here: 58.7 us
  Pallas kernels  31.8 us (54%)
  starting transfers between devices  22.6 us (38%)
  waiting for transfers between devices  3.23 us (5%)
  between operations  1 us (2%)
    pallas_call x8, Pallas kernels, call(): run(*[at_home(x, spec) for x, spec in zip(args, specs)])  31.8 us
    all_to_all x2, starting transfers between devices, exchange(): return lax.all_to_all(value, axes, split_axis=0, concat_axis=0, tiled=True)  17.9 us
    ppermute x4, starting transfers between devices, swapped(): return lax.ppermute(value, axes, pairs + [(b, a) for a, b in pairs])  4.67 us
    all_to_all x2, waiting for transfers between devices, exchange(): return lax.all_to_all(value, axes, split_axis=0, concat_axis=0, tiled=True)  3.22 us
  transfers between devices with their start and end apart: 6, of which 2 were waited for; matrix products, arithmetic and copies ran while one was open for 0% of the time, Pallas kernels for 38%

profile of v4, /device:TPU:32, one launch (start us, length us, event | category | flops | bytes accessed | tf_op | source)
XLA Modules:
  0.0 58.7 jit_solution(10708093491800516065)
XLA Ops:
  0.6 1.1 %line_ends.1 = (f32[96,128]{1,0:T(8,128)S(1)}, f32[96,128]{1,0:T(8,128)S(1)}) custom-call(f32[40,256,128]{2,1,0:T(8,128)} %w_hbm.7, f32[12,256,128]{2,1,0:T(8,128)} %pool_hbm.5), custom_call_target="tpu_custom_call" | custom-call | tf_op jit(solution)/shard_map/line_ends/pallas_call | solution.py:452
  1.8 0.1 collective-permute-start
  1.9 0.7 %collective-permute-start.1 = (f32[96,128]{1,0:T(8,128)S(1)}, f32[96,128]{1,0:T(8,128)S(1)}, u32[]{:S(2)}, u32[]{:S(2)}) collective-permute-start(f32[96,128]{1,0:T(8,128)S(1)} %get-tuple-element.20.row_b.rest_3_), channel_id=1, source_target_pairs={{32,64},{96,128},{160,192},{64,32},{128,96},{192,160},{33,65},{97,... | collective-permute-start | bytes 147464 | tf_op jit(solution)/shard_map/ppermute | solution.py:466
  2.6 4.9 %column_ends.1 = (f32[96,256]{1,0:T(8,128)S(1)}, f32[96,256]{1,0:T(8,128)S(1)}, f32[40,256,128]{2,1,0:T(8,128)S(1)}, f32[12,256,128]{2,1,0:T(8,128)S(1)}) custom-call(f32[40,256,128]{2,1,0:T(8,128)} %w_hbm.7, f32[12,256,128]{2,1,0:T(8,128)} %pool_hbm.5), custom_call_target="tpu_custom_call" | custom-call | tf_op jit(solution)/shard_map/column_ends/pallas_call | solution.py:452
  7.5 0.0 collective-permute-done.row_a_got.rest_4_
  7.5 0.0 collective-permute-done.1.row_b_got.rest_5_
  7.6 3.8 %collective-permute-start.3 = (f32[136,256]{1,0:T(8,128)S(1)}, f32[136,256]{1,0:T(8,128)S(1)}, u32[]{:S(2)}, u32[]{:S(2)}) collective-permute-start(f32[136,256]{1,0:T(8,128)S(1)} %get-tuple-element.30), channel_id=1, source_target_pairs={{1,2},{3,4},{5,6},{7,8},{9,10},{11,12},{13,14},{15,16},{17,18},{19... | collective-permute-start | bytes 417800 | tf_op jit(solution)/shard_map/ppermute | solution.py:466
  11.4 0.1 collective-permute-start.2
  11.5 0.0 copy-start
  11.5 0.0 copy-start.1
  11.5 5.1 %gram.1 = (f32[12,128]{1,0:T(8,128)S(1)}, f32[12,256,128]{2,1,0:T(8,128)}) custom-call(f32[40,256,128]{2,1,0:T(8,128)S(1)} %get-tuple-element.16.w_ref, f32[12,256,128]{2,1,0:T(8,128)S(1)} %get-tuple-element.17.pool_ref), custom_call_target="tpu_custom_call" | custom-call | tf_op jit(solution)/shard_map/gram/pallas_call | solution.py:452
  16.6 0.0 collective-permute-done.3.col_b_got.rest_9_
  16.6 0.0 collective-permute-done.2.col_a_got.rest_8_
  16.6 1.0 %cross.1 = f32[16,1,1536]{2,1,0:T(1,128)} custom-call(f32[12,128]{1,0:T(8,128)S(1)} %get-tuple-element.18.sums_ref, f32[96,128]{1,0:T(8,128)S(1)} %get-tuple-element.19.row_a.rest_2_, f32[96,128]{1,0:T(8,128)S(1)} %get-tuple-element.20.row_b.rest_3_, f32[96,128]{1,0:T(8,128)S(1)} %collective-permute-done.row_a_got.rest_4_, ...), custom_call_target="tpu_custom_call" | custom-call | tf_op jit(solution)/shard_map/cross/pallas_call | solution.py:452
  17.6 10.6 %all-to-all-start = ((f32[16,1,1536]{2,1,0:T(1,128)}), f32[16,1,1536]{2,1,0:T(1,128)S(1)}, u32[]{:S(2)}, u32[]{:S(2)}) async-start(f32[16,1,1536]{2,1,0:T(1,128)} %cross.1), calls=%async_computation | async-start | bytes 196608 | tf_op jit(solution)/shard_map/all_to_all | solution.py:470
  28.2 0.0 copy-done
  28.2 0.0 copy-done.1
  28.2 5.9 %base.2 = (f32[16,256,128]{2,1,0:T(8,128)}, f32[12,256,128]{2,1,0:T(8,128)}, f32[40,8,256]{2,1,0:T(8,128)S(1)}, f32[2,256,128]{2,1,0:T(8,128)S(1)}) custom-call(f32[40]{0:T(128)S(1)} %copy-done, s32[40]{0:T(128)S(1)} %copy-done.1, f32[40,256,128]{2,1,0:T(8,128)} %w_hbm.7, f32[12,256,128]{2,1,0:T(8,128)} %get-tuple-element.23.lap_in_hbm, ...), custom_call_target="tpu_custom_call" | custom-call | tf_op jit(solution)/shard_map/base/pallas_call | solution.py:452
  34.1 1.6 %all-to-all-done.parts_ref = f32[16,1,1536]{2,1,0:T(1,128)S(1)} async-done(((f32[16,1,1536]{2,1,0:T(1,128)}), f32[16,1,1536]{2,1,0:T(1,128)S(1)}, u32[]{:S(2)}, u32[]{:S(2)}) %all-to-all-start) | async-done | bytes 98336 | tf_op jit(solution)/shard_map/all_to_all | solution.py:470
  35.7 0.7 %again.1 = f32[16,1,1536]{2,1,0:T(1,128)} custom-call(f32[16,1,1536]{2,1,0:T(1,128)S(1)} %all-to-all-done.parts_ref, f32[2,256,128]{2,1,0:T(8,128)S(1)} %get-tuple-element.24.token_ref.rest_1_), custom_call_target="tpu_custom_call" | custom-call | tf_op jit(solution)/shard_map/again/pallas_call | solution.py:452
  36.4 7.3 %all-to-all-start.1 = ((f32[16,1,1536]{2,1,0:T(1,128)}), f32[16,1,1536]{2,1,0:T(1,128)S(1)}, u32[]{:S(2)}, u32[]{:S(2)}) async-start(f32[16,1,1536]{2,1,0:T(1,128)} %again.1), calls=%async_computation.1 | async-start | bytes 196608 | tf_op jit(solution)/shard_map/all_to_all | solution.py:470
  43.7 0.0 copy-start.2
  43.7 0.0 copy-start.3
  43.7 0.0 copy-start.4
  43.7 0.0 copy-start.5
  43.7 6.1 %base.3.base_b_hbm = f32[24,256,128]{2,1,0:T(8,128)} custom-call(f32[40]{0:T(128)S(1)} %copy-done, s32[40]{0:T(128)S(1)} %copy-done.1, f32[40,256,128]{2,1,0:T(8,128)} %w_hbm.7, f32[12,256,128]{2,1,0:T(8,128)} %get-tuple-element.23.lap_in_hbm, f32[40,8,256]{2,1,0:T(8,128)S(1)} %get-tuple-element.26.rest_0_, ...), custom_call_target="tpu_custom_call" | custom-call | tf_op jit(solution)/shard_map/base/pallas_call | solution.py:452
  49.9 1.6 %all-to-all-done.1.parts_ref = f32[16,1,1536]{2,1,0:T(1,128)S(1)} async-done(((f32[16,1,1536]{2,1,0:T(1,128)}), f32[16,1,1536]{2,1,0:T(1,128)S(1)}, u32[]{:S(2)}, u32[]{:S(2)}) %all-to-all-start.1) | async-done | bytes 98336 | tf_op jit(solution)/shard_map/all_to_all | solution.py:470
  51.5 0.0 copy-done.2
  51.5 0.0 copy-done.3
  51.5 0.0 copy-done.4
  51.5 0.0 copy-done.5
  51.5 7.0 %finish.1 = (f32[40,256,128]{2,1,0:T(8,128)}, f32[2,16,40]{2,1,0:T(8,128)}) custom-call(f32[16,1,1536]{2,1,0:T(1,128)S(1)} %all-to-all-done.1.parts_ref, f32[8,12]{1,0:T(8,128)S(1)} %bitcast.10, s32[2,16]{1,0:T(2,128)S(1)} %copy-done.3, s32[1,40]{1,0:T(1,128)S(1)} %bitcast.11, f32[1,40]{1,0:T(1,128)S(1)} %bitcast.12, f32[1,40]{1,0:T(1,128)S(1)} %bitcast.7, ...), custom_call_target="tpu_custom_call" | custom-call | tf_op jit(solution)/shard_map/finish/pallas_call | solution.py:452
  (3 shorter events, 0.0 us)
Async XLA Ops:
  1.8 5.7 %collective-permute-start = (f32[96,128]{1,0:T(8,128)S(1)}, f32[96,128]{1,0:T(8,128)S(1)}, u32[]{:S(2)}, u32[]{:S(2)}) collective-permute-start(f32[96,128]{1,0:T(8,128)S(1)} %get-tuple-element.19.row_a.rest_2_), channel_id=1, source_target_pairs={{0,32},{64,96},{128,160},{192,224},{32,0},{96,64},{160,128},{224,1... | collective-permute-start | bytes 147464 | tf_op jit(solution)/shard_map/ppermute | solution.py:466
  1.9 5.6 %collective-permute-start.1 = (f32[96,128]{1,0:T(8,128)S(1)}, f32[96,128]{1,0:T(8,128)S(1)}, u32[]{:S(2)}, u32[]{:S(2)}) collective-permute-start(f32[96,128]{1,0:T(8,128)S(1)} %get-tuple-element.20.row_b.rest_3_), channel_id=1, source_target_pairs={{32,64},{96,128},{160,192},{64,32},{128,96},{192,160},{33,65},{97,... | collective-permute-start | bytes 147464 | tf_op jit(solution)/shard_map/ppermute | solution.py:466
  7.6 9.0 %collective-permute-start.3 = (f32[136,256]{1,0:T(8,128)S(1)}, f32[136,256]{1,0:T(8,128)S(1)}, u32[]{:S(2)}, u32[]{:S(2)}) collective-permute-start(f32[136,256]{1,0:T(8,128)S(1)} %get-tuple-element.30), channel_id=1, source_target_pairs={{1,2},{3,4},{5,6},{7,8},{9,10},{11,12},{13,14},{15,16},{17,18},{19... | collective-permute-start | bytes 417800 | tf_op jit(solution)/shard_map/ppermute | solution.py:466
  11.4 5.2 %collective-permute-start.2 = (f32[136,256]{1,0:T(8,128)S(1)}, f32[136,256]{1,0:T(8,128)S(1)}, u32[]{:S(2)}, u32[]{:S(2)}) collective-permute-start(f32[136,256]{1,0:T(8,128)S(1)} %get-tuple-element.31), channel_id=1, source_target_pairs={{0,1},{2,3},{4,5},{6,7},{8,9},{10,11},{12,13},{14,15},{16,17},{18,... | collective-permute-start | bytes 417800 | tf_op jit(solution)/shard_map/ppermute | solution.py:466
  11.5 16.7 %copy-start = (f32[40]{0:T(128)S(1)}, f32[40]{0:T(128)}, u32[]{:S(2)}) copy-start(f32[40]{0:T(128)} %smooth_ref.3) | copy-start | bytes 484
  11.5 16.7 %copy-start.1 = (s32[40]{0:T(128)S(1)}, s32[40]{0:T(128)}, u32[]{:S(2)}) copy-start(s32[40]{0:T(128)} %active_ref.3) | copy-start | bytes 484
  17.6 18.2 %all-to-all-start = ((f32[16,1,1536]{2,1,0:T(1,128)}), f32[16,1,1536]{2,1,0:T(1,128)S(1)}, u32[]{:S(2)}, u32[]{:S(2)}) async-start(f32[16,1,1536]{2,1,0:T(1,128)} %cross.1), calls=%async_computation | async-start | bytes 196608 | tf_op jit(solution)/shard_map/all_to_all | solution.py:470
  36.4 15.1 %all-to-all-start.1 = ((f32[16,1,1536]{2,1,0:T(1,128)}), f32[16,1,1536]{2,1,0:T(1,128)S(1)}, u32[]{:S(2)}, u32[]{:S(2)}) async-start(f32[16,1,1536]{2,1,0:T(1,128)} %again.1), calls=%async_computation.1 | async-start | bytes 196608 | tf_op jit(solution)/shard_map/all_to_all | solution.py:470
  43.7 7.8 %copy-start.2 = (f32[12,8]{0,1:T(8,128)S(1)}, f32[12,8]{0,1:T(8,128)}, u32[]{:S(2)}) copy-start(f32[12,8]{0,1:T(8,128)} %param.10) | copy-start | bytes 1156
  43.7 7.8 %copy-start.3 = (s32[2,16]{1,0:T(2,128)S(1)}, s32[2,16]{1,0:T(2,128)}, u32[]{:S(2)}) copy-start(s32[2,16]{1,0:T(2,128)} %plan_ref.1) | copy-start | bytes 388
  43.7 7.8 %copy-start.4 = (s32[40]{0:T(128)S(1)}, s32[40]{0:T(128)}, u32[]{:S(2)}) copy-start(s32[40]{0:T(128)} %param.12) | copy-start | bytes 484
  43.7 7.8 %copy-start.5 = (f32[40]{0:T(128)S(1)}, f32[40]{0:T(128)}, u32[]{:S(2)}) copy-start(f32[40]{0:T(128)} %param.13) | copy-start | bytes 484

commit v5 on v4

--- a/solution.py
+++ b/solution.py
@@ -427,7 +427,7 @@
         store(t).start()
         return carry
 
-    lax.fori_loop(0, 8, step, 0)
+    lax.fori_loop(0, 8, step, 0, unroll=2)
     for t, e in enumerate((e0, e1)):
         err_ref[t] = dot(hits[t], e, TN, EXACT)
     for t in range(8):

time: 59 us -> 59.1 us (level)
  no operation moved by 1% of the time
where the time goes in v5:
time: 59.1 us; the launch traced here: 58.7 us
  Pallas kernels  31.8 us (54%)
  starting transfers between devices  22.6 us (38%)
  waiting for transfers between devices  3.23 us (5%)
  between operations  1 us (2%)
    pallas_call x8, Pallas kernels, call(): run(*[at_home(x, spec) for x, spec in zip(args, specs)])  31.8 us
    all_to_all x2, starting transfers between devices, exchange(): return lax.all_to_all(value, axes, split_axis=0, concat_axis=0, tiled=True)  17.9 us
    ppermute x4, starting transfers between devices, swapped(): return lax.ppermute(value, axes, pairs + [(b, a) for a, b in pairs])  4.67 us
    all_to_all x2, waiting for transfers between devices, exchange(): return lax.all_to_all(value, axes, split_axis=0, concat_axis=0, tiled=True)  3.22 us
  transfers between devices with their start and end apart: 6, of which 2 were waited for; matrix products, arithmetic and copies ran while one was open for 0% of the time, Pallas kernels for 38%

profile of v5, /device:TPU:32, one launch (start us, length us, event | category | flops | bytes accessed | tf_op | source)
XLA Modules:
  0.0 58.7 jit_solution(1751765772179235832)
XLA Ops:
  0.6 1.1 %line_ends.1 = (f32[96,128]{1,0:T(8,128)S(1)}, f32[96,128]{1,0:T(8,128)S(1)}) custom-call(f32[40,256,128]{2,1,0:T(8,128)} %w_hbm.7, f32[12,256,128]{2,1,0:T(8,128)} %pool_hbm.5), custom_call_target="tpu_custom_call" | custom-call | tf_op jit(solution)/shard_map/line_ends/pallas_call | solution.py:452
  1.8 0.1 collective-permute-start
  1.9 0.7 %collective-permute-start.1 = (f32[96,128]{1,0:T(8,128)S(1)}, f32[96,128]{1,0:T(8,128)S(1)}, u32[]{:S(2)}, u32[]{:S(2)}) collective-permute-start(f32[96,128]{1,0:T(8,128)S(1)} %get-tuple-element.20.row_b.rest_3_), channel_id=1, source_target_pairs={{32,64},{96,128},{160,192},{64,32},{128,96},{192,160},{33,65},{97,... | collective-permute-start | bytes 147464 | tf_op jit(solution)/shard_map/ppermute | solution.py:466
  2.6 4.9 %column_ends.1 = (f32[96,256]{1,0:T(8,128)S(1)}, f32[96,256]{1,0:T(8,128)S(1)}, f32[40,256,128]{2,1,0:T(8,128)S(1)}, f32[12,256,128]{2,1,0:T(8,128)S(1)}) custom-call(f32[40,256,128]{2,1,0:T(8,128)} %w_hbm.7, f32[12,256,128]{2,1,0:T(8,128)} %pool_hbm.5), custom_call_target="tpu_custom_call" | custom-call | tf_op jit(solution)/shard_map/column_ends/pallas_call | solution.py:452
  7.5 0.0 collective-permute-done.row_a_got.rest_4_
  7.5 0.0 collective-permute-done.1.row_b_got.rest_5_
  7.6 3.8 %collective-permute-start.3 = (f32[136,256]{1,0:T(8,128)S(1)}, f32[136,256]{1,0:T(8,128)S(1)}, u32[]{:S(2)}, u32[]{:S(2)}) collective-permute-start(f32[136,256]{1,0:T(8,128)S(1)} %get-tuple-element.30), channel_id=1, source_target_pairs={{1,2},{3,4},{5,6},{7,8},{9,10},{11,12},{13,14},{15,16},{17,18},{19... | collective-permute-start | bytes 417800 | tf_op jit(solution)/shard_map/ppermute | solution.py:466
  11.4 0.1 collective-permute-start.2
  11.5 0.0 copy-start
  11.5 0.0 copy-start.1
  11.5 5.1 %gram.1 = (f32[12,128]{1,0:T(8,128)S(1)}, f32[12,256,128]{2,1,0:T(8,128)}) custom-call(f32[40,256,128]{2,1,0:T(8,128)S(1)} %get-tuple-element.16.w_ref, f32[12,256,128]{2,1,0:T(8,128)S(1)} %get-tuple-element.17.pool_ref), custom_call_target="tpu_custom_call" | custom-call | tf_op jit(solution)/shard_map/gram/pallas_call | solution.py:452
  16.6 0.0 collective-permute-done.3.col_b_got.rest_9_
  16.6 0.0 collective-permute-done.2.col_a_got.rest_8_
  16.6 1.0 %cross.1 = f32[16,1,1536]{2,1,0:T(1,128)} custom-call(f32[12,128]{1,0:T(8,128)S(1)} %get-tuple-element.18.sums_ref, f32[96,128]{1,0:T(8,128)S(1)} %get-tuple-element.19.row_a.rest_2_, f32[96,128]{1,0:T(8,128)S(1)} %get-tuple-element.20.row_b.rest_3_, f32[96,128]{1,0:T(8,128)S(1)} %collective-permute-done.row_a_got.rest_4_, ...), custom_call_target="tpu_custom_call" | custom-call | tf_op jit(solution)/shard_map/cross/pallas_call | solution.py:452
  17.6 10.6 %all-to-all-start = ((f32[16,1,1536]{2,1,0:T(1,128)}), f32[16,1,1536]{2,1,0:T(1,128)S(1)}, u32[]{:S(2)}, u32[]{:S(2)}) async-start(f32[16,1,1536]{2,1,0:T(1,128)} %cross.1), calls=%async_computation | async-start | bytes 196608 | tf_op jit(solution)/shard_map/all_to_all | solution.py:470
  28.2 0.0 copy-done
  28.2 0.0 copy-done.1
  28.2 5.9 %base.2 = (f32[16,256,128]{2,1,0:T(8,128)}, f32[12,256,128]{2,1,0:T(8,128)}, f32[40,8,256]{2,1,0:T(8,128)S(1)}, f32[2,256,128]{2,1,0:T(8,128)S(1)}) custom-call(f32[40]{0:T(128)S(1)} %copy-done, s32[40]{0:T(128)S(1)} %copy-done.1, f32[40,256,128]{2,1,0:T(8,128)} %w_hbm.7, f32[12,256,128]{2,1,0:T(8,128)} %get-tuple-element.23.lap_in_hbm, ...), custom_call_target="tpu_custom_call" | custom-call | tf_op jit(solution)/shard_map/base/pallas_call | solution.py:452
  34.1 1.6 %all-to-all-done.parts_ref = f32[16,1,1536]{2,1,0:T(1,128)S(1)} async-done(((f32[16,1,1536]{2,1,0:T(1,128)}), f32[16,1,1536]{2,1,0:T(1,128)S(1)}, u32[]{:S(2)}, u32[]{:S(2)}) %all-to-all-start) | async-done | bytes 98336 | tf_op jit(solution)/shard_map/all_to_all | solution.py:470
  35.7 0.7 %again.1 = f32[16,1,1536]{2,1,0:T(1,128)} custom-call(f32[16,1,1536]{2,1,0:T(1,128)S(1)} %all-to-all-done.parts_ref, f32[2,256,128]{2,1,0:T(8,128)S(1)} %get-tuple-element.24.token_ref.rest_1_), custom_call_target="tpu_custom_call" | custom-call | tf_op jit(solution)/shard_map/again/pallas_call | solution.py:452
  36.4 7.3 %all-to-all-start.1 = ((f32[16,1,1536]{2,1,0:T(1,128)}), f32[16,1,1536]{2,1,0:T(1,128)S(1)}, u32[]{:S(2)}, u32[]{:S(2)}) async-start(f32[16,1,1536]{2,1,0:T(1,128)} %again.1), calls=%async_computation.1 | async-start | bytes 196608 | tf_op jit(solution)/shard_map/all_to_all | solution.py:470
  43.7 0.0 copy-start.2
  43.7 0.0 copy-start.3
  43.7 0.0 copy-start.4
  43.7 0.0 copy-start.5
  43.7 6.1 %base.3.base_b_hbm = f32[24,256,128]{2,1,0:T(8,128)} custom-call(f32[40]{0:T(128)S(1)} %copy-done, s32[40]{0:T(128)S(1)} %copy-done.1, f32[40,256,128]{2,1,0:T(8,128)} %w_hbm.7, f32[12,256,128]{2,1,0:T(8,128)} %get-tuple-element.23.lap_in_hbm, f32[40,8,256]{2,1,0:T(8,128)S(1)} %get-tuple-element.26.rest_0_, ...), custom_call_target="tpu_custom_call" | custom-call | tf_op jit(solution)/shard_map/base/pallas_call | solution.py:452
  49.9 1.6 %all-to-all-done.1.parts_ref = f32[16,1,1536]{2,1,0:T(1,128)S(1)} async-done(((f32[16,1,1536]{2,1,0:T(1,128)}), f32[16,1,1536]{2,1,0:T(1,128)S(1)}, u32[]{:S(2)}, u32[]{:S(2)}) %all-to-all-start.1) | async-done | bytes 98336 | tf_op jit(solution)/shard_map/all_to_all | solution.py:470
  51.5 0.0 copy-done.2
  51.5 0.0 copy-done.3
  51.5 0.0 copy-done.4
  51.5 0.0 copy-done.5
  51.5 7.0 %finish.1 = (f32[40,256,128]{2,1,0:T(8,128)}, f32[2,16,40]{2,1,0:T(8,128)}) custom-call(f32[16,1,1536]{2,1,0:T(1,128)S(1)} %all-to-all-done.1.parts_ref, f32[8,12]{1,0:T(8,128)S(1)} %bitcast.10, s32[2,16]{1,0:T(2,128)S(1)} %copy-done.3, s32[1,40]{1,0:T(1,128)S(1)} %bitcast.11, f32[1,40]{1,0:T(1,128)S(1)} %bitcast.12, f32[1,40]{1,0:T(1,128)S(1)} %bitcast.7, ...), custom_call_target="tpu_custom_call" | custom-call | tf_op jit(solution)/shard_map/finish/pallas_call | solution.py:452
  (3 shorter events, 0.0 us)
Async XLA Ops:
  1.8 5.7 %collective-permute-start = (f32[96,128]{1,0:T(8,128)S(1)}, f32[96,128]{1,0:T(8,128)S(1)}, u32[]{:S(2)}, u32[]{:S(2)}) collective-permute-start(f32[96,128]{1,0:T(8,128)S(1)} %get-tuple-element.19.row_a.rest_2_), channel_id=1, source_target_pairs={{0,32},{64,96},{128,160},{192,224},{32,0},{96,64},{160,128},{224,1... | collective-permute-start | bytes 147464 | tf_op jit(solution)/shard_map/ppermute | solution.py:466
  1.9 5.6 %collective-permute-start.1 = (f32[96,128]{1,0:T(8,128)S(1)}, f32[96,128]{1,0:T(8,128)S(1)}, u32[]{:S(2)}, u32[]{:S(2)}) collective-permute-start(f32[96,128]{1,0:T(8,128)S(1)} %get-tuple-element.20.row_b.rest_3_), channel_id=1, source_target_pairs={{32,64},{96,128},{160,192},{64,32},{128,96},{192,160},{33,65},{97,... | collective-permute-start | bytes 147464 | tf_op jit(solution)/shard_map/ppermute | solution.py:466
  7.6 9.0 %collective-permute-start.3 = (f32[136,256]{1,0:T(8,128)S(1)}, f32[136,256]{1,0:T(8,128)S(1)}, u32[]{:S(2)}, u32[]{:S(2)}) collective-permute-start(f32[136,256]{1,0:T(8,128)S(1)} %get-tuple-element.30), channel_id=1, source_target_pairs={{1,2},{3,4},{5,6},{7,8},{9,10},{11,12},{13,14},{15,16},{17,18},{19... | collective-permute-start | bytes 417800 | tf_op jit(solution)/shard_map/ppermute | solution.py:466
  11.4 5.2 %collective-permute-start.2 = (f32[136,256]{1,0:T(8,128)S(1)}, f32[136,256]{1,0:T(8,128)S(1)}, u32[]{:S(2)}, u32[]{:S(2)}) collective-permute-start(f32[136,256]{1,0:T(8,128)S(1)} %get-tuple-element.31), channel_id=1, source_target_pairs={{0,1},{2,3},{4,5},{6,7},{8,9},{10,11},{12,13},{14,15},{16,17},{18,... | collective-permute-start | bytes 417800 | tf_op jit(solution)/shard_map/ppermute | solution.py:466
  11.5 16.7 %copy-start = (f32[40]{0:T(128)S(1)}, f32[40]{0:T(128)}, u32[]{:S(2)}) copy-start(f32[40]{0:T(128)} %smooth_ref.3) | copy-start | bytes 484
  11.5 16.7 %copy-start.1 = (s32[40]{0:T(128)S(1)}, s32[40]{0:T(128)}, u32[]{:S(2)}) copy-start(s32[40]{0:T(128)} %active_ref.3) | copy-start | bytes 484
  17.6 18.2 %all-to-all-start = ((f32[16,1,1536]{2,1,0:T(1,128)}), f32[16,1,1536]{2,1,0:T(1,128)S(1)}, u32[]{:S(2)}, u32[]{:S(2)}) async-start(f32[16,1,1536]{2,1,0:T(1,128)} %cross.1), calls=%async_computation | async-start | bytes 196608 | tf_op jit(solution)/shard_map/all_to_all | solution.py:470
  36.4 15.1 %all-to-all-start.1 = ((f32[16,1,1536]{2,1,0:T(1,128)}), f32[16,1,1536]{2,1,0:T(1,128)S(1)}, u32[]{:S(2)}, u32[]{:S(2)}) async-start(f32[16,1,1536]{2,1,0:T(1,128)} %again.1), calls=%async_computation.1 | async-start | bytes 196608 | tf_op jit(solution)/shard_map/all_to_all | solution.py:470
  43.7 7.8 %copy-start.2 = (f32[12,8]{0,1:T(8,128)S(1)}, f32[12,8]{0,1:T(8,128)}, u32[]{:S(2)}) copy-start(f32[12,8]{0,1:T(8,128)} %param.10) | copy-start | bytes 1156
  43.7 7.8 %copy-start.3 = (s32[2,16]{1,0:T(2,128)S(1)}, s32[2,16]{1,0:T(2,128)}, u32[]{:S(2)}) copy-start(s32[2,16]{1,0:T(2,128)} %plan_ref.1) | copy-start | bytes 388
  43.7 7.8 %copy-start.4 = (s32[40]{0:T(128)S(1)}, s32[40]{0:T(128)}, u32[]{:S(2)}) copy-start(s32[40]{0:T(128)} %param.12) | copy-start | bytes 484
  43.7 7.8 %copy-start.5 = (f32[40]{0:T(128)S(1)}, f32[40]{0:T(128)}, u32[]{:S(2)}) copy-start(f32[40]{0:T(128)} %param.13) | copy-start | bytes 484
